TPU v7x, 32 devices: a whole 2x2x4 slice. The times are simulated.
32 devices in a mesh: fsdp: 8 (over z, y), seq: 4 (over x, core).
Axes of the slice: x: 2, y: 2, z: 4, core: 2. Of those that a mesh axis runs over, the one named last changes fastest.
Arguments:
- tokens: bfloat16 [8, 512, 4096], P('fsdp'), may hold values from -7 to 7
- norm_gain: float32 [4096], replicated, may hold values from 0.1 to 1.9
- curvature: bfloat16 [8, 512, 4096], P('fsdp'), may hold values from 0.19921875 to 2
- weight_slots: bfloat16 [4, 400, 128, 128], P('seq', 'fsdp'), may hold values from -1 to 1
- probe_slots: bfloat16 [4, 400, 128, 128], P('seq', 'fsdp'), may hold values from -0.09375 to 0.09375
- block_counts: int32 [4, 8], P('seq'), may hold values from 1 to 50, 320 in all within a row
Outputs:
- hvp_slots: float32 [4, 400, 128, 128], P('seq', 'fsdp')
Inputs may be any that keep to these rules, and one draw needn't show every extreme that they name: `block_counts`: in each row, device d along fsdp owns the n_d blocks that follow the earlier devices' blocks, in its first n_d slots; a row sums to 320, and 50 is reached in every row.
All inputs are finite; a program needn't handle non-finite values.
Results may differ from a plain program's by a relative error of at most 0.018.
Values may be sent and summed in bfloat16 or wider, within the bound.
A program may use at most 128 MiB of HBM per device.

v0:
```python
import functools

import jax
import jax.numpy as jnp
from jax import lax
from jax.experimental import pallas as pl
from jax.experimental.pallas import tpu as pltpu
from jax.sharding import PartitionSpec as P

D = 4096
HQ = 16
HK = 4
HD = 128
BLK = 128


THETA = 500000.0
EPS = 1e-05
NEGATIVE = -1e30


def rotary(length, head_dim):
    half_dim = head_dim // 2
    frequency = jnp.exp(-jnp.log(THETA) * 2.0 * jnp.arange(half_dim, dtype=jnp.float32) / head_dim)
    angles = jnp.arange(length, dtype=jnp.float32)[:, None] * frequency[None, :]
    return (jnp.cos(angles)[:, None, :], jnp.sin(angles)[:, None, :])


def rotate(field_in, cosine, sine):
    half_dim = field_in.shape[-1] // 2
    first_half = field_in[..., :half_dim]
    second = field_in[..., half_dim:]
    return jnp.concatenate(
        [first_half * cosine - second * sine, second * cosine + first_half * sine], axis=-1
    )


VMEM_BYTES = 62 * 1024 * 1024


def attention(projected, cosine, sine, q_heads, kv_heads):
    length = projected.shape[0]
    head_dim = projected.shape[1] // (q_heads + 2 * kv_heads)
    q_end = q_heads * head_dim
    k_end = q_end + kv_heads * head_dim
    queries = rotate(projected[:, :q_end].reshape(length, q_heads, head_dim), cosine, sine).astype(
        jnp.bfloat16
    )
    key_rows = rotate(
        projected[:, q_end:k_end].reshape(length, kv_heads, head_dim), cosine, sine
    ).astype(jnp.bfloat16)
    values = projected[:, k_end:].reshape(length, kv_heads, head_dim).astype(jnp.bfloat16)
    queries = queries.reshape(length, kv_heads, q_heads // kv_heads, head_dim)
    scores = jnp.einsum(
        "qkgd,skd->kgqs", queries, key_rows, preferred_element_type=jnp.float32
    ) * head_dim ** (-0.5)
    causal = jnp.arange(length)[:, None] >= jnp.arange(length)[None, :]
    scores = jnp.where(causal, scores, NEGATIVE)
    attn_probs = jax.nn.softmax(scores, axis=-1).astype(jnp.bfloat16)
    mixed_heads = jnp.einsum(
        "kgqs,skd->qkgd", attn_probs, values, preferred_element_type=jnp.float32
    )
    return mixed_heads.reshape(length, q_heads * head_dim).astype(jnp.bfloat16)


def ring_position(index, n):
    odd = lax.rem(index, 2)
    half = lax.div(index, 2)
    return (1 - odd) * half + odd * (n - 1 - half)


def ring_index(position, n):
    back = lax.div(position, n // 2)
    return (1 - back) * 2 * position + back * (2 * (n - 1 - position) + 1)


def pieces(slots):
    half = slots // 2
    out = []
    for direction, first, count in ((0, 0, half), (1, half, slots - half)):
        cuts = 5 if count % 5 == 0 else 1
        size = count // cuts
        out.append([(first + i * size, size) for i in range(cuts)])
    return out


def enter(neighbours, axis="fsdp"):
    barrier = pltpu.get_barrier_semaphore()
    for neighbour in neighbours:
        pl.semaphore_signal(
            barrier, inc=1, device_id={axis: neighbour}, device_id_type=pl.DeviceIdType.MESH
        )
    pl.semaphore_wait(barrier, len(neighbours))


def gather_kernel(n, slots, grid_qkv, grid_out, slot_ref, w_ref, p_ref, tokens_ref, gain_ref,
                  proj_ref, d_proj_ref, wo_ref, po_ref, normed_t_ref, held_w, held_p, matrix,
                  normed, send_sem, recv_sem):
    me = lax.axis_index("fsdp")
    pos = ring_position(me, n)
    right = ring_index(lax.rem(pos + 1, n), n)
    left = ring_index(lax.rem(pos + n - 1, n), n)
    towards = (right, left)
    enter((left, right))
    parts = pieces(slots)
    arrays = ((w_ref, held_w), (p_ref, held_p))

    def copy(which, step, direction, j):
        own, held = arrays[which]
        first, size = parts[direction][j]
        shift = n - step if direction == 0 else step
        origin = ring_index(lax.rem(pos + shift, n), n)
        there = held.at[pl.ds(origin * slots + first, size)]
        here = own.at[pl.ds(first, size)] if step == 0 else there
        return pltpu.make_async_remote_copy(
            src_ref=here,
            dst_ref=there,
            send_sem=send_sem.at[which, step, direction, j],
            recv_sem=recv_sem.at[which, step, direction, j],
            device_id={"fsdp": towards[direction]},
            device_id_type=pl.DeviceIdType.MESH,
        )

    def arrival(which, step, direction, j):
        first, size = parts[direction][j]
        own, held = arrays[which]
        shift = n - step - 1 if direction == 0 else step + 1
        origin = ring_index(lax.rem(pos + shift, n), n)
        there = held.at[pl.ds(origin * slots + first, size)]
        pltpu.make_async_remote_copy(
            src_ref=there,
            dst_ref=there,
            send_sem=send_sem.at[which, step, direction, j],
            recv_sem=recv_sem.at[which, step, direction, j],
            device_id={"fsdp": towards[direction]},
            device_id_type=pl.DeviceIdType.MESH,
        ).wait_recv()

    def each():
        for j in range(max(len(parts[0]), len(parts[1]))):
            for direction in range(2):
                if j < len(parts[direction]):
                    yield direction, j

    def normalize():
        rows = 32

        def some(i, carry):
            here = pl.ds(pl.multiple_of(i * rows, rows), rows)
            values = tokens_ref[here, :].astype(jnp.float32)
            factor = lax.rsqrt(jnp.mean(values * values, axis=-1, keepdims=True) + EPS)
            normed[here, :] = (values * factor * gain_ref[...]).astype(jnp.bfloat16)
            return carry

        lax.fori_loop(0, normed.shape[0] // rows, some, 0)

    def transpose():
        edge = held_w.shape[-1]

        def some(i, carry):
            here = pl.ds(pl.multiple_of(i * edge, edge), edge)
            normed_t_ref[here, :] = normed[:, here].T
            return carry

        lax.fori_loop(0, normed.shape[1] // edge, some, 0)

    def project(result_ref):
        rows = 256

        def some(i, carry):
            here = pl.ds(pl.multiple_of(i * rows, rows), rows)
            result_ref[here, :] = jnp.dot(
                normed[here, :], matrix[...], preferred_element_type=jnp.float32
            )
            return carry

        lax.fori_loop(0, normed.shape[0] // rows, some, 0)

    def unpack(which, qkv_ref, out_ref):
        own, held = arrays[which]
        rows, cols = grid_qkv
        edge = held.shape[-1]

        def qkv_row(i, carry):
            for c in range(cols):
                qkv_ref[pl.ds(pl.multiple_of(i * edge, edge), edge), c * edge:(c + 1) * edge] = (
                    held[slot_ref[i * cols + c]]
                )
            return carry

        lax.fori_loop(0, rows, qkv_row, 0)
        out_rows, out_cols = grid_out

        def out_col(i, carry):
            for r in range(out_rows):
                out_ref[r * edge:(r + 1) * edge, pl.ds(pl.multiple_of(i * edge, edge), edge)] = (
                    held[slot_ref[rows * cols + r * out_cols + i]]
                )
            return carry

        lax.fori_loop(0, out_cols, out_col, 0)

    def finish(which, qkv_ref, out_ref):
        own, held = arrays[which]
        for direction, j in each():
            arrival(which, n - 2, direction, j)
        held[pl.ds(me * slots, slots)] = own[...]
        unpack(which, qkv_ref, out_ref)

    sent = []
    for which in range(2):
        for step in range(n - 1):
            for direction, j in each():
                if step > 0:
                    arrival(which, step - 1, direction, j)
                one = copy(which, step, direction, j)
                one.start()
                sent.append(one)
            if which == 0 and step == 0:
                normalize()
            if which == 0 and step == 1:
                transpose()
            if which == 1 and step == 0:
                finish(0, matrix, wo_ref)
            if which == 1 and step == 1:
                project(proj_ref)
    finish(1, matrix, po_ref)
    project(d_proj_ref)
    for one in sent:
        one.wait_send()


def gather_weights(slot_of, weights, probes, tokens, gain, n, grid_qkv, grid_out):
    slots, edge, _ = weights.shape
    cuts = max(len(part) for part in pieces(slots))
    length, width = tokens.shape
    proj = jax.ShapeDtypeStruct((length, grid_qkv[1] * edge), jnp.float32)
    turned = jax.ShapeDtypeStruct((width, length), jnp.bfloat16)
    out = jax.ShapeDtypeStruct((grid_out[0] * edge, grid_out[1] * edge), jnp.bfloat16)
    vmem = pl.BlockSpec(memory_space=pltpu.VMEM)
    return pl.pallas_call(
        functools.partial(gather_kernel, n, slots, grid_qkv, grid_out),
        out_shape=(proj, proj, out, out, turned),
        in_specs=[pl.BlockSpec(memory_space=pltpu.SMEM)] + [vmem] * 4,
        out_specs=(vmem,) * 5,
        scratch_shapes=[
            pltpu.VMEM((n * slots, edge, edge), jnp.bfloat16),
            pltpu.VMEM((n * slots, edge, edge), jnp.bfloat16),
            pltpu.VMEM((grid_qkv[0] * edge, grid_qkv[1] * edge), jnp.bfloat16),
            pltpu.VMEM((length, width), jnp.bfloat16),
            pltpu.SemaphoreType.DMA((2, n - 1, 2, cuts)),
            pltpu.SemaphoreType.DMA((2, n - 1, 2, cuts)),
        ],
        compiler_params=pltpu.CompilerParams(
            collective_id=0, has_side_effects=True, vmem_limit_bytes=VMEM_BYTES
        ),
    )(slot_of, weights, probes, tokens, gain)


def gradient_blocks(grid_qkv, grid_out, normed_t_ref, d_proj_ref, mixed_t_ref, weighted_ref,
                    out_ref):
    edge = out_ref.shape[-1]
    rows, cols = grid_qkv
    out_rows, out_cols = grid_out
    group = 2

    out_ref[rows * cols + out_rows * out_cols] = jnp.zeros((edge, edge), out_ref.dtype)

    def qkv_rows(i, carry):
        width = group * edge
        left = normed_t_ref[pl.ds(pl.multiple_of(i * width, width), width), :]
        block = jnp.dot(
            left, d_proj_ref[...], preferred_element_type=jnp.float32
        ).astype(jnp.bfloat16)
        for r in range(group):
            for c in range(cols):
                out_ref[(i * group + r) * cols + c] = block[
                    r * edge:(r + 1) * edge, c * edge:(c + 1) * edge
                ]
        return carry

    lax.fori_loop(0, rows // group, qkv_rows, 0)

    def out_columns(i, carry):
        width = group * edge
        right = weighted_ref[:, pl.ds(pl.multiple_of(i * width, width), width)]
        block = jnp.dot(
            mixed_t_ref[...], right, preferred_element_type=jnp.float32
        ).astype(jnp.bfloat16)
        for r in range(out_rows):
            for c in range(group):
                out_ref[rows * cols + r * out_cols + i * group + c] = block[
                    r * edge:(r + 1) * edge, c * edge:(c + 1) * edge
                ]
        return carry

    lax.fori_loop(0, out_cols // group, out_columns, 0)


def reduce_kernel(n, slots, scale, grid_qkv, grid_out, pick_ref, normed_t_ref, d_proj_ref,
                  mixed_t_ref, weighted_ref, out_ref, grads, begin, held, send_sem, recv_sem):
    me = lax.axis_index("fsdp")
    pos = ring_position(me, n)
    right = ring_index(lax.rem(pos + 1, n), n)
    left = ring_index(lax.rem(pos + n - 1, n), n)
    towards = (right, left)
    enter((left, right))
    parts = pieces(slots)
    gradient_blocks(
        grid_qkv, grid_out, normed_t_ref, d_proj_ref, mixed_t_ref, weighted_ref, grads
    )

    def own(step, direction, j):
        shift = n - 1 - step if direction == 0 else 1 + step
        target = ring_index(lax.rem(pos + shift, n), n)
        return target * slots

    def each_block(direction, j, body):
        first, size = parts[direction][j]

        def some(i, carry):
            body(first + i)
            return carry

        lax.fori_loop(0, size, some, 0)

    def copy(step, direction, j):
        first, size = parts[direction][j]
        here = begin.at[pl.ds(first, size)] if step == 0 else held.at[step - 1, pl.ds(first, size)]
        return pltpu.make_async_remote_copy(
            src_ref=here,
            dst_ref=held.at[step, pl.ds(first, size)],
            send_sem=send_sem.at[step, direction, j],
            recv_sem=recv_sem.at[step, direction, j],
            device_id={"fsdp": towards[direction]},
            device_id_type=pl.DeviceIdType.MESH,
        )

    def each():
        for j in range(max(len(parts[0]), len(parts[1]))):
            for direction in range(2):
                if j < len(parts[direction]):
                    yield direction, j

    sent = {}
    for step in range(n - 1):
        for direction, j in each():
            first, size = parts[direction][j]
            base = own(step, direction, j)
            if step > 0:
                sent[step - 1, direction, j].wait_recv()

                def add(t, step=step, base=base):
                    held[step - 1, t] = (
                        held[step - 1, t].astype(jnp.float32)
                        + grads[pick_ref[base + t]].astype(jnp.float32)
                    ).astype(jnp.bfloat16)

                each_block(direction, j, add)
            else:

                def fill(t, base=base):
                    begin[t] = grads[pick_ref[base + t]]

                each_block(direction, j, fill)
            one = copy(step, direction, j)
            one.start()
            sent[step, direction, j] = one
    for direction, j in each():
        first, size = parts[direction][j]
        sent[n - 2, direction, j].wait_recv()
        base = own(n - 1, direction, j)

        def last(t, base=base):
            out_ref[t] = (
                held[n - 2, t].astype(jnp.float32) + grads[pick_ref[base + t]].astype(jnp.float32)
            ) * scale

        each_block(direction, j, last)
    for one in sent.values():
        one.wait_send()


def reduce_slots(picked, normed_t, d_proj, mixed_t, weighted, n, scale, grid_qkv, grid_out):
    slots = picked.shape[0] // n
    edge = BLK
    total_blocks = grid_qkv[0] * grid_qkv[1] + grid_out[0] * grid_out[1]
    cuts = max(len(part) for part in pieces(slots))
    vmem = pl.BlockSpec(memory_space=pltpu.VMEM)
    return pl.pallas_call(
        functools.partial(reduce_kernel, n, slots, scale, grid_qkv, grid_out),
        out_shape=jax.ShapeDtypeStruct((slots, edge, edge), jnp.float32),
        in_specs=[pl.BlockSpec(memory_space=pltpu.SMEM)] + [vmem] * 4,
        out_specs=vmem,
        scratch_shapes=[
            pltpu.VMEM((total_blocks + 1, edge, edge), jnp.bfloat16),
            pltpu.VMEM((slots, edge, edge), jnp.bfloat16),
            pltpu.VMEM((n - 1, slots, edge, edge), jnp.bfloat16),
            pltpu.SemaphoreType.DMA((n - 1, 2, cuts)),
            pltpu.SemaphoreType.DMA((n - 1, 2, cuts)),
        ],
        compiler_params=pltpu.CompilerParams(
            collective_id=1, has_side_effects=True, vmem_limit_bytes=VMEM_BYTES
        ),
    )(picked, normed_t, d_proj, mixed_t, weighted)


def exchange_kernel(mixed_ref, d_mixed_ref, w_ref, p_ref, curv_ref, weighted_ref, back_ref,
                    terms, near, pair, far, share, rest, send_sem, recv_sem):
    me = lax.axis_index("seq")
    side = lax.rem(me, 2)
    core = me + 1 - 2 * side
    across = me + 2 - 4 * lax.rem(lax.div(me, 2), 2)
    enter((core, across), "seq")
    length, width = terms.shape
    half = width // 2
    chunks = recv_sem.shape[1]
    rows = length // chunks
    mine = pl.ds(pl.multiple_of(side * half, half), half)
    other = pl.ds(pl.multiple_of((1 - side) * half, half), half)

    def block(i):
        return pl.ds(i * rows, rows)

    def copy(stage, i, here, there, target):
        return pltpu.make_async_remote_copy(
            src_ref=here,
            dst_ref=there,
            send_sem=send_sem.at[stage, i],
            recv_sem=recv_sem.at[stage, i],
            device_id={"seq": target},
            device_id_type=pl.DeviceIdType.MESH,
        )

    def terms_of(i):
        tile = width // 4

        def columns(j, carry):
            cols = pl.ds(pl.multiple_of(j * tile, tile), tile)
            terms[block(i), cols] = (
                jnp.dot(d_mixed_ref[block(i), :], w_ref[:, cols], preferred_element_type=jnp.float32)
                + jnp.dot(mixed_ref[block(i), :], p_ref[:, cols], preferred_element_type=jnp.float32)
            ).astype(jnp.bfloat16)
            return carry

        lax.fori_loop(0, 4, columns, 0)

    first = [copy(0, i, terms.at[block(i), other], near.at[block(i)], core) for i in range(chunks)]
    second = [copy(1, i, pair.at[block(i)], far.at[block(i)], across) for i in range(chunks)]
    third = [copy(2, i, share.at[block(i)], rest.at[block(i)], core) for i in range(chunks)]

    def send_pair(i):
        first[i].wait_recv()
        pair[block(i)] = (
            terms[block(i), mine].astype(jnp.float32) + near[block(i)].astype(jnp.float32)
        ).astype(jnp.bfloat16)
        second[i].start()

    def send_share(i):
        second[i].wait_recv()
        total = pair[block(i)].astype(jnp.float32) + far[block(i)].astype(jnp.float32)
        share[block(i)] = (curv_ref[block(i), mine].astype(jnp.float32) * total).astype(
            jnp.bfloat16
        )
        third[i].start()

    def finish(i):
        weighted_ref[block(i), mine] = share[block(i)]
        third[i].wait_recv()
        weighted_ref[block(i), other] = rest[block(i)]
        back_ref[block(i), :] = lax.dot_general(
            weighted_ref[block(i), :],
            w_ref[...],
            (((1,), (1,)), ((), ())),
            preferred_element_type=jnp.float32,
        ).astype(jnp.bfloat16)

    for i in range(chunks):
        terms_of(i)
        first[i].start()
        if i > 0:
            send_pair(i - 1)
    send_pair(chunks - 1)
    for i in range(chunks):
        send_share(i)
        if i > 0:
            finish(i - 1)
    finish(chunks - 1)
    for one in first + second + third:
        one.wait_send()


def exchange(mixed, d_mixed, w_out, p_out, curvature):
    length, width = curvature.shape
    chunks = 4
    vmem = pl.BlockSpec(memory_space=pltpu.VMEM)
    half = pltpu.VMEM((length, width // 2), jnp.bfloat16)
    return pl.pallas_call(
        exchange_kernel,
        out_shape=(
            jax.ShapeDtypeStruct((length, width), jnp.bfloat16),
            jax.ShapeDtypeStruct(mixed.shape, jnp.bfloat16),
        ),
        in_specs=[vmem] * 5,
        out_specs=(vmem, vmem),
        scratch_shapes=[
            pltpu.VMEM((length, width), jnp.bfloat16),
            half,
            half,
            half,
            half,
            half,
            pltpu.SemaphoreType.DMA((3, chunks)),
            pltpu.SemaphoreType.DMA((3, chunks)),
        ],
        compiler_params=pltpu.CompilerParams(
            collective_id=2, has_side_effects=True, vmem_limit_bytes=VMEM_BYTES
        ),
    )(mixed, d_mixed, w_out, p_out, curvature)


def local(tokens, norm_gain, curvature, weight_slots, probe_slots, block_counts):
    n_columns = lax.axis_size("seq")
    n_owners = lax.axis_size("fsdp")
    q_heads = HQ // n_columns
    kv_heads = HK // n_columns
    row_blocks = D // BLK
    qkv_cols = (q_heads + 2 * kv_heads) * HD // BLK
    out_rows = q_heads * HD // BLK
    grid_qkv, grid_out = (row_blocks, qkv_cols), (out_rows, row_blocks)
    total_blocks = row_blocks * qkv_cols + out_rows * row_blocks
    slots = weight_slots.shape[1]
    length = tokens.shape[1]
    counts = block_counts[0]
    range_ends = jnp.cumsum(counts)
    starts = range_ends - counts
    owner_ids = jnp.arange(n_owners, dtype=jnp.int32)
    block_ids = jnp.arange(total_blocks, dtype=jnp.int32)
    owners = jnp.sum((range_ends[None, :] <= block_ids[:, None]).astype(jnp.int32), axis=1)
    first_block = jnp.sum(
        jnp.where(owners[:, None] == owner_ids[None, :], starts[None, :], 0), axis=1
    )
    slot_of = (owners * slots + block_ids - first_block).astype(jnp.int32)
    projected, d_projected, w_out, p_out, normed_t = gather_weights(
        slot_of,
        weight_slots[0],
        probe_slots[0],
        tokens[0],
        norm_gain[None, :],
        n_owners,
        grid_qkv,
        grid_out,
    )
    cosine, sine = rotary(length, HD)

    def inner(projected):
        return attention(projected, cosine, sine, q_heads, kv_heads)

    mixed, d_mixed = jax.jvp(inner, (projected,), (d_projected,))
    weighted, back_mixed = exchange(mixed, d_mixed, w_out, p_out, curvature[0])
    mixed_again, pullback = jax.vjp(inner, projected)
    (back_projected,) = pullback(back_mixed)
    slot_index = jnp.arange(n_owners * slots, dtype=jnp.int32)
    place = slot_index % slots
    owner_hot = (slot_index // slots)[:, None] == owner_ids[None, :]
    owner_first = jnp.sum(jnp.where(owner_hot, starts[None, :], 0), axis=1)
    own_count = jnp.sum(jnp.where(owner_hot, counts[None, :], 0), axis=1)
    picked = jnp.where(place < own_count, owner_first + place, total_blocks).astype(jnp.int32)
    scaled = reduce_slots(
        picked,
        normed_t,
        back_projected.astype(jnp.bfloat16),
        mixed_again.T,
        weighted,
        n_owners,
        (length * n_owners) ** -0.5,
        grid_qkv,
        grid_out,
    )
    return scaled.reshape(1, slots, BLK, BLK)


def solution(mesh):
    in_specs = (
        P("fsdp", None, None),
        P(),
        P("fsdp", None, None),
        P("seq", "fsdp", None, None),
        P("seq", "fsdp", None, None),
        P("seq", None),
    )
    out_specs = P("seq", "fsdp", None, None)
    return jax.shard_map(local, mesh=mesh, in_specs=in_specs, out_specs=out_specs, check_vma=False)
```

profile of v0, /device:TPU:1, one launch (start us, length us, event | category | flops | bytes accessed | tf_op | source)
XLA Modules:
  0.0 519.8 jit_solution(1161910811117251182)
XLA Ops:
  0.0 0.8 reduce-window.4
  0.8 0.1 convert_reduce_fusion
  0.9 0.7 fusion.76
  1.6 0.1 select_reduce_fusion.2
  1.7 0.6 add_subtract_fusion.slot_ref
  2.2 0.0 copy-done.16
  2.3 266.9 %shard_map.64 = (f32[512,768]{1,0:T(8,128)}, f32[512,768]{1,0:T(8,128)}, bf16[512,4096]{1,0:T(8,128)(2,1)}, bf16[512,4096]{1,0:T(8,128)(2,1)}, bf16[4096,512]{1,0:T(8,128)(2,1)}) custom-call(s32[320]{0:T(512)} %add_subtract_fusion.slot_ref, bf16[50,128,128]{2,1,0:T(8,128)(2,1)} %bitcast.204, bf16[50,128,128]{2,1,0:T(8,128)(2,1)} %bitcast.205, ...), custom_call_target="tpu_custom_call" | custom-call | tf_op jit(solution)/shard_map/pallas_call | solution.py:241
  269.2 1.3 slice.55
  270.5 0.4 reshape.292
  270.9 1.3 slice.62
  272.2 0.4 reshape.295
  272.5 1.2 fusion.88
  273.8 1.0 fusion.57
  274.8 0.5 subtract_convert_fusion
  275.3 1.3 slice_bitcast_fusion
  276.6 1.4 fusion.68
  278.0 0.8 fusion.63
  278.8 0.1 iota_compare_fusion
  278.9 1.2 fusion.10
  280.1 2.1 fusion.90
  282.2 0.9 fusion.87
  283.1 2.8 fusion.11
  285.9 1.0 divide_convert_fusion
  286.9 0.0 copy-start.2
  286.9 1.6 fusion.22
  288.5 1.0 copy.62.d_mixed_ref
  289.5 1.4 fusion.26
  291.0 1.0 copy.38.mixed_ref
  291.9 0.0 copy-done.2
  292.0 63.7 %shard_map.65 = (bf16[512,4096]{1,0:T(8,128)(2,1)}, bf16[512,512]{1,0:T(8,128)(2,1)}) custom-call(bf16[512,512]{1,0:T(8,128)(2,1)} %copy.38.mixed_ref, bf16[512,512]{1,0:T(8,128)(2,1)} %copy.62.d_mixed_ref, bf16[512,4096]{1,0:T(8,128)(2,1)} %get-tuple-element.15.w_ref, bf16[512,4096]{1,0:T(8,128)(2,1)} %get-tuple-element.16.p_ref, bf16[512,4096]{1,0:T(8,128)(2,1)} %bitcast.200), custom_call_target="tpu_custom_call" | custom-call | tf_op jit(solution)/shard_map/pallas_call | solution.py:498
  355.7 0.0 copy-done.3
  355.7 1.3 copy.63
  356.9 2.3 fusion.44
  359.3 4.0 fusion.8
  363.3 2.1 fusion.50
  365.4 0.0 copy-done.15
  365.5 1.4 multiply_add_fusion.3
  366.8 0.1 add_bitcast_fusion.1
  367.0 2.1 fusion.25
  369.2 0.0 copy-start.18
  369.2 0.5 multiply_add_fusion.1
  369.7 0.3 copy_bitcast_fusion
  370.0 1.0 add_convert_fusion.2.d_proj_ref
  371.0 0.0 copy-done.18
  371.0 0.1 select_reduce_fusion.1
  371.1 0.6 add_select_fusion.2.pick_ref
  371.7 144.1 %shard_map.66 = f32[50,128,128]{2,1,0:T(8,128)} custom-call(s32[400]{0:T(512)} %add_select_fusion.2.pick_ref, bf16[4096,512]{1,0:T(8,128)(2,1)} %get-tuple-element.12.normed_t_ref, bf16[512,768]{1,0:T(8,128)(2,1)} %add_convert_fusion.2.d_proj_ref, bf16[512,512]{1,0:T(8,128)(2,1)} %bitcast.198, bf16[512,4096]{1,0:T(8,128)(2,1)} %get-tuple-element.18.weighted_ref), custom_call_target="tpu_custom_call" | custom-call | tf_op jit(solution)/shard_map/pallas_call | solution.py:390
  515.8 4.0 copy.82
  (36 shorter events, 0.1 us)
Async XLA Ops:
  1.6 0.7 copy-start.16
  273.8 2.8 copy-start.14
  274.7 3.2 copy-start.6
  274.8 3.2 copy-start.8
  275.3 3.6 copy-start.4
  278.0 2.1 copy-start.10
  280.1 5.8 %copy-start = (f32[512,512,4]{1,0,2:T(8,128)}, f32[512,512,4]{1,0,2:T(8,128)S(1)}, u32[]{:S(2)}) copy-start(f32[512,512,4]{1,0,2:T(8,128)S(1)} %get-tuple-element.44) | copy-start | bytes 12582916
  283.1 2.8 copy-start.12
  286.9 5.1 copy-start.2
  291.0 64.7 %copy-start.3 = (bf16[128,4,512]{2,0,1:T(8,128)(2,1)}, bf16[128,4,512]{2,0,1:T(8,128)(2,1)S(1)}, u32[]{:S(2)}) copy-start(bf16[128,4,512]{2,0,1:T(8,128)(2,1)S(1)} %fusion.26) | copy-start | bytes 1572868
  292.0 67.3 %copy-start.13 = (f32[4,512]{1,0:T(4,128)S(1)}, f32[4,512]{1,0:T(4,128)}, u32[]{:S(2)}) copy-start(f32[4,512]{1,0:T(4,128)} %copy-done.12) | copy-start | bytes 24580
  359.2 4.0 copy-start.1
  359.3 4.0 copy-start.5
  363.3 2.2 copy-start.15
  363.3 3.7 copy-start.11
  367.0 2.2 copy-start.7
  367.0 2.2 copy-start.9
  369.2 1.8 copy-start.17
  369.2 1.8 copy-start.18
where the time goes:
time: 521 us; the launch traced here: 520 us
  Pallas kernels  475 us (91%)
  matrix products  20.4 us (4%)
  local copies, waits for them, and re-layouts  13.1 us (3%)
  other arithmetic  11.1 us (2%)
    pallas_call x1, Pallas kernels, gather_weights(): pl.pallas_call(functools.partial(gather_kernel, n, slots, grid_qkv, grid_...  267 us
    pallas_call x1, Pallas kernels, reduce_slots(): pl.pallas_call(functools.partial(reduce_kernel, n, slots, scale, grid_qkv...  144 us
    pallas_call x1, Pallas kernels, exchange(): pl.pallas_call(exchange_kernel, out_shape=(jax.ShapeDtypeStruct((length,...  63.7 us
    dot_general x5, matrix products, attention(): jnp.einsum('kgqs,skd->qkgd', attn_probs, values, preferred_element_type=j...  12 us

commit v1 on v0

--- a/solution.py
+++ b/solution.py
@@ -36,6 +36,7 @@
 
 
 VMEM_BYTES = 62 * 1024 * 1024
+GRID_VMEM_BYTES = 67043328
 
 
 def attention(projected, cosine, sine, q_heads, kv_heads):
@@ -580,6 +581,851 @@
     return scaled.reshape(1, slots, BLK, BLK)
 
 
+def spot():
+    f = lax.axis_index("fsdp")
+    s = lax.axis_index("seq")
+    return lax.div(f, 2), lax.rem(f, 2), lax.div(s, 2), lax.rem(s, 2)
+
+
+def device(z, y, x, c):
+    return {"fsdp": 2 * z + y, "seq": 2 * x + c}
+
+
+def mirrored(z, c, planes):
+    return z + c * (planes - 1 - 2 * z)
+
+
+def greet(peers):
+    barrier = pltpu.get_barrier_semaphore()
+    for peer in peers:
+        pl.semaphore_signal(barrier, inc=1, device_id=peer, device_id_type=pl.DeviceIdType.MESH)
+    pl.semaphore_wait(barrier, len(peers))
+
+
+def shard_columns(x, j, width):
+    return x * (width // 4) + j * (width // 8), width // 2 + j * (width // 4) + x * (width // 8)
+
+
+def cut_count(slots):
+    return 5 if slots % 5 == 0 else 1
+
+
+def gather_grid_kernel(n, slots, grid_qkv, grid_out, slot_ref, w_ref, p_ref, tokens_ref, gain_ref,
+                       curv_ref, proj_ref, d_proj_ref, wo_ref, po_ref, normed_t_ref, curv_out_ref,
+                       held_w, held_p, matrix, normed, curv_part, send_y, send_core, send_z, recv, tok_send,
+                       tok_recv, relay_send, relay_recv, curv_send, curv_recv):
+    planes = n // 2
+    z, y, x, c = spot()
+    zeta = mirrored(z, c, planes)
+    hub = lax.rem(zeta, 2) == 0
+    spoke = lax.rem(zeta, 2) == 1
+    mate = z + 1 - 2 * lax.rem(z, 2)
+    y_peer = device(z, 1 - y, x, c)
+    x_peer = device(z, y, 1 - x, c)
+    core_peer = device(z, y, x, 1 - c)
+    z_peer = device(mate, y, x, c)
+    row = [device(lax.rem(z + i, planes), y, x, c) for i in range(1, planes)]
+    greet(row + [core_peer, y_peer, x_peer])
+    cuts = cut_count(slots)
+    size = slots // cuts
+    own = (w_ref, p_ref)
+    held = (held_w, held_p)
+    me = 2 * z + y
+    tok_cuts = tok_send.shape[0]
+    half = normed.shape[0] // 2
+    tok_rows = half // tok_cuts
+    width = normed.shape[1]
+    part = width // 8
+
+    def at(zeta_at):
+        return mirrored(zeta_at, c, planes)
+
+    def spread(which, d, j):
+        return held[which].at[pl.ds(d * slots + j * size, size)]
+
+    def move(src, which, d, j, peer, sem):
+        return pltpu.make_async_remote_copy(
+            src_ref=src,
+            dst_ref=spread(which, d, j),
+            send_sem=sem,
+            recv_sem=recv.at[d, which * cuts + j],
+            device_id=peer,
+            device_id_type=pl.DeviceIdType.MESH,
+        )
+
+    def own_chunk(which, j):
+        return own[which].at[pl.ds(j * size, size)]
+
+    def arrive(which, d, j):
+        move(spread(which, d, j), which, d, j, core_peer, send_y.at[0, 0]).wait_recv()
+
+    other_hub = device(at(2 - zeta), y, x, c)
+    near_hub = device(at(2), y, x, c)
+    end_hub = device(at(0), y, x, c)
+
+    def token_copy(i, rows_half, peer, s_sem, r_sem, src):
+        rows = pl.ds(rows_half * half + i * tok_rows, tok_rows)
+        return pltpu.make_async_remote_copy(
+            src_ref=src.at[rows],
+            dst_ref=normed.at[rows],
+            send_sem=s_sem.at[i],
+            recv_sem=r_sem.at[i],
+            device_id=peer,
+            device_id_type=pl.DeviceIdType.MESH,
+        )
+
+    def curv_copy(i):
+        first = shard_columns(x, lax.rem(mate, 2), width)[i]
+        return pltpu.make_async_remote_copy(
+            src_ref=curv_ref.at[:, pl.ds(pl.multiple_of(first, part), part)],
+            dst_ref=curv_part.at[i],
+            send_sem=curv_send.at[i],
+            recv_sem=curv_recv.at[i],
+            device_id=z_peer,
+            device_id_type=pl.DeviceIdType.MESH,
+        )
+
+    def curv_local(i):
+        first = shard_columns(x, lax.rem(z, 2), width)[i]
+        return pltpu.make_async_copy(
+            curv_ref.at[:, pl.ds(pl.multiple_of(first, part), part)],
+            curv_part.at[i],
+            curv_recv.at[i],
+        )
+
+    def to_z(which, j):
+        k = which * cuts + j
+        return move(own_chunk(which, j), which, me, j, other_hub, send_z.at[0, k])
+
+    def to_y(which, j):
+        k = which * cuts + j
+        return move(own_chunk(which, j), which, me, j, y_peer, send_y.at[0, k])
+
+    def to_core(which, j):
+        k = which * cuts + j
+        return move(own_chunk(which, j), which, me, j, core_peer, send_core.at[0, k])
+
+    def spoke_own(which, j):
+        src = own_chunk(which, j)
+        k = which * cuts + j
+        return (
+            move(src, which, me, j, near_hub, send_z.at[0, k]),
+            move(src, which, me, j, end_hub, send_z.at[1, k]),
+        )
+
+    lead = min(2, 2 * cuts)
+    every = [(which, j) for which in range(2) for j in range(cuts)]
+
+    @pl.when(hub)
+    def _():
+        for k in range(lead):
+            to_y(*every[k]).start()
+        for k, one in enumerate(every):
+            to_z(*one).start()
+            if k < tok_cuts:
+                token_copy(k, x, z_peer, tok_send, tok_recv, tokens_ref).start()
+            to_core(*one).start()
+        for k in range(len(every), tok_cuts):
+            token_copy(k, x, z_peer, tok_send, tok_recv, tokens_ref).start()
+        for i in range(2):
+            curv_copy(i).start()
+            curv_local(i).start()
+
+    @pl.when(spoke)
+    def _():
+        for one in every:
+            for copy in spoke_own(*one):
+                copy.start()
+
+    def pass_row(k):
+        which, j = every[k]
+        for r in range(1, planes):
+            d = 2 * at(lax.rem(zeta + r, planes)) + y
+            arrive(which, d, j)
+            src = spread(which, d, j)
+            move(src, which, d, j, y_peer, send_y.at[r, k]).start()
+            move(src, which, d, j, core_peer, send_core.at[r, k]).start()
+            if r == 1 and k + lead < len(every):
+                to_y(*every[k + lead]).start()
+
+    def pass_across(k):
+        which, j = every[k]
+        for r in range(planes):
+            d = 2 * at(lax.rem(zeta + r, planes)) + 1 - y
+            arrive(which, d, j)
+            move(spread(which, d, j), which, d, j, core_peer, send_core.at[planes + r, k]).start()
+
+    def forward(which, j):
+        k = which * cuts + j
+        pass_row(k)
+        if k not in (0, cuts):
+            pass_across(k - 1)
+        if k in (cuts - 1, 2 * cuts - 1):
+            pass_across(k)
+
+    def step(which, j):
+        @pl.when(hub)
+        def _():
+            forward(which, j)
+
+        @pl.when(spoke)
+        def _():
+            for d in range(n):
+                arrive(which, d, j)
+
+    def normalize(source):
+        rows = 32
+
+        def some(i, carry):
+            here = pl.ds(pl.multiple_of(i * rows, rows), rows)
+            values = source[here, :].astype(jnp.float32)
+            factor = lax.rsqrt(jnp.mean(values * values, axis=-1, keepdims=True) + EPS)
+            normed[here, :] = (values * factor * gain_ref[...]).astype(jnp.bfloat16)
+            return carry
+
+        lax.fori_loop(0, normed.shape[0] // rows, some, 0)
+
+    def transpose():
+        edge = held_w.shape[-1]
+
+        def some(i, carry):
+            here = pl.ds(pl.multiple_of(i * edge, edge), edge)
+            normed_t_ref[here, :] = normed[:, here].T
+            return carry
+
+        lax.fori_loop(0, normed.shape[1] // edge, some, 0)
+
+    def project(result_ref):
+        rows = 256
+
+        def some(i, carry):
+            here = pl.ds(pl.multiple_of(i * rows, rows), rows)
+            result_ref[here, :] = jnp.dot(
+                normed[here, :], matrix[...], preferred_element_type=jnp.float32
+            )
+            return carry
+
+        lax.fori_loop(0, normed.shape[0] // rows, some, 0)
+
+    def unpack_qkv(which):
+        rows, cols = grid_qkv
+        edge = held_w.shape[-1]
+
+        def qkv_row(i, carry):
+            for col in range(cols):
+                matrix[pl.ds(pl.multiple_of(i * edge, edge), edge), col * edge:(col + 1) * edge] = (
+                    held[which][slot_ref[i * cols + col]]
+                )
+            return carry
+
+        lax.fori_loop(0, rows, qkv_row, 0)
+
+    def unpack_out(which, out_ref):
+        rows, cols = grid_qkv
+        out_rows, out_cols = grid_out
+        edge = held_w.shape[-1]
+
+        def out_col(i, carry):
+            for r in range(out_rows):
+                out_ref[r * edge:(r + 1) * edge, pl.ds(pl.multiple_of(i * edge, edge), edge)] = (
+                    held[which][slot_ref[rows * cols + r * out_cols + i]]
+                )
+            return carry
+
+        lax.fori_loop(0, out_cols, out_col, 0)
+
+    def keep_own(which):
+        @pl.when(hub)
+        def _():
+            held[which][pl.ds(me * slots, slots)] = own[which][...]
+
+    @pl.when(hub)
+    def _():
+        normalize(tokens_ref)
+
+    @pl.when(spoke)
+    def _():
+        for i in range(tok_cuts):
+            token_copy(i, x, z_peer, tok_send, tok_recv, normed).wait_recv()
+            token_copy(i, x, x_peer, relay_send, relay_recv, normed).start()
+        for i in range(tok_cuts):
+            token_copy(i, 1 - x, x_peer, relay_send, relay_recv, normed).wait_recv()
+        for i in range(tok_cuts):
+            token_copy(i, x, x_peer, relay_send, relay_recv, normed).wait_send()
+        normalize(normed)
+
+    for j in range(cuts):
+        step(0, j)
+        if j == 0:
+            transpose()
+    keep_own(0)
+    todo = [
+        lambda: unpack_qkv(0),
+        lambda: project(proj_ref),
+        lambda: unpack_out(0, wo_ref),
+    ]
+    for j in range(cuts):
+        step(1, j)
+        if j < cuts - 1 and todo:
+            todo.pop(0)()
+    while todo:
+        todo.pop(0)()
+    keep_own(1)
+    unpack_qkv(1)
+    project(d_proj_ref)
+    unpack_out(1, po_ref)
+
+    @pl.when(hub)
+    def _():
+        for i in range(2):
+            curv_local(i).wait()
+
+    @pl.when(spoke)
+    def _():
+        for i in range(2):
+            curv_copy(i).wait_recv()
+
+    curv_out_ref[...] = curv_part[...]
+
+    @pl.when(hub)
+    def _():
+        for i in range(tok_cuts):
+            token_copy(i, x, z_peer, tok_send, tok_recv, tokens_ref).wait_send()
+        for i in range(2):
+            curv_copy(i).wait_send()
+        for k, (which, j) in enumerate(every):
+            to_z(which, j).wait_send()
+            to_y(which, j).wait_send()
+            to_core(which, j).wait_send()
+            src = spread(which, me, j)
+            for r in range(1, planes):
+                move(src, which, me, j, y_peer, send_y.at[r, k]).wait_send()
+            for r in range(1, n):
+                move(src, which, me, j, core_peer, send_core.at[r, k]).wait_send()
+
+    @pl.when(spoke)
+    def _():
+        for one in every:
+            for copy in spoke_own(*one):
+                copy.wait_send()
+
+
+def gather_grid(slot_of, weights, probes, tokens, gain, curvature, n, grid_qkv, grid_out):
+    slots, edge, _ = weights.shape
+    cuts = cut_count(slots)
+    length, width = tokens.shape
+    proj = jax.ShapeDtypeStruct((length, grid_qkv[1] * edge), jnp.float32)
+    turned = jax.ShapeDtypeStruct((width, length), jnp.bfloat16)
+    out = jax.ShapeDtypeStruct((grid_out[0] * edge, grid_out[1] * edge), jnp.bfloat16)
+    shard = (2, length, width // 8)
+    vmem = pl.BlockSpec(memory_space=pltpu.VMEM)
+    dma = pltpu.SemaphoreType.DMA
+    return pl.pallas_call(
+        functools.partial(gather_grid_kernel, n, slots, grid_qkv, grid_out),
+        out_shape=(proj, proj, out, out, turned, jax.ShapeDtypeStruct(shard, jnp.bfloat16)),
+        in_specs=[pl.BlockSpec(memory_space=pltpu.SMEM)] + [vmem] * 4
+        + [pl.BlockSpec(memory_space=pl.ANY)],
+        out_specs=(vmem,) * 6,
+        scratch_shapes=[
+            pltpu.VMEM((n * slots, edge, edge), jnp.bfloat16),
+            pltpu.VMEM((n * slots, edge, edge), jnp.bfloat16),
+            pltpu.VMEM((grid_qkv[0] * edge, grid_qkv[1] * edge), jnp.bfloat16),
+            pltpu.VMEM((length, width), jnp.bfloat16),
+            pltpu.VMEM(shard, jnp.bfloat16),
+            dma((n // 2, 2 * cuts)),
+            dma((n, 2 * cuts)),
+            dma((2, 2 * cuts)),
+            dma((n, 2 * cuts)),
+            dma((4,)),
+            dma((4,)),
+            dma((4,)),
+            dma((4,)),
+            dma((2,)),
+            dma((2,)),
+        ],
+        compiler_params=pltpu.CompilerParams(
+            collective_id=3, has_side_effects=True, vmem_limit_bytes=GRID_VMEM_BYTES
+        ),
+    )(slot_of, weights, probes, tokens, gain, curvature)
+
+
+def square_kernel(mixed_ref, d_mixed_ref, w_ref, p_ref, curv_ref, weighted_ref, back_ref, terms,
+                  near_x, near_z, pair_a, pair_b, far_z, far_x, full, send_sem, recv_sem):
+    z, y, x, c = spot()
+    side = lax.rem(z, 2)
+    x_peer = device(z, y, 1 - x, c)
+    z_peer = device(z + 1 - 2 * side, y, x, c)
+    greet([x_peer, z_peer])
+    length, width = terms.shape
+    quarter, part = width // 4, width // 8
+    chunks = recv_sem.shape[1]
+    rows = length // chunks
+
+    def block(i):
+        return pl.ds(i * rows, rows)
+
+    def cols(first, count):
+        return pl.ds(pl.multiple_of(first, count), count)
+
+    keep_a, give_a = cols(x * quarter, quarter), cols((1 - x) * quarter, quarter)
+    keep_b = cols(width // 2 + side * quarter, quarter)
+    give_b = cols(width // 2 + (1 - side) * quarter, quarter)
+    first_a, first_b = shard_columns(x, side, width)
+    own_a, own_b = cols(first_a, part), cols(first_b, part)
+
+    def copy(kind, i, here, there, target):
+        return pltpu.make_async_remote_copy(
+            src_ref=here,
+            dst_ref=there,
+            send_sem=send_sem.at[kind, i],
+            recv_sem=recv_sem.at[kind, i],
+            device_id=target,
+            device_id_type=pl.DeviceIdType.MESH,
+        )
+
+    def stage(i):
+        b = block(i)
+        return (
+            copy(0, i, terms.at[b, give_a], near_x.at[b], x_peer),
+            copy(1, i, terms.at[b, give_b], near_z.at[b], z_peer),
+            copy(2, i, pair_a.at[b, cols((1 - side) * part, part)], far_z.at[b], z_peer),
+            copy(3, i, pair_b.at[b, cols((1 - x) * part, part)], far_x.at[b], x_peer),
+            copy(4, i, full.at[b, own_a], full.at[b, own_a], z_peer),
+            copy(5, i, full.at[b, own_b], full.at[b, own_b], x_peer),
+            copy(6, i, full.at[b, keep_a], full.at[b, keep_a], x_peer),
+            copy(7, i, full.at[b, keep_b], full.at[b, keep_b], z_peer),
+        )
+
+    def incoming(kind, i, there):
+        copy(kind, i, there, there, x_peer).wait_recv()
+
+    def terms_of(i):
+        tile = width // 4
+
+        def columns(j, carry):
+            here = pl.ds(pl.multiple_of(j * tile, tile), tile)
+            terms[block(i), here] = (
+                jnp.dot(d_mixed_ref[block(i), :], w_ref[:, here], preferred_element_type=jnp.float32)
+                + jnp.dot(mixed_ref[block(i), :], p_ref[:, here], preferred_element_type=jnp.float32)
+            ).astype(jnp.bfloat16)
+            return carry
+
+        lax.fori_loop(0, 4, columns, 0)
+
+    plans = [stage(i) for i in range(chunks)]
+
+    def pair_up(i):
+        b = block(i)
+        for kind, pair, keep, near in ((0, pair_a, keep_a, near_x), (1, pair_b, keep_b, near_z)):
+            incoming(kind, i, near.at[b])
+            pair[b] = (
+                terms[b, keep].astype(jnp.float32) + near[b].astype(jnp.float32)
+            ).astype(jnp.bfloat16)
+            plans[i][2 + kind].start()
+
+    def weigh(i):
+        b = block(i)
+        for kind, pair, mine, far, own_cols in (
+            (0, pair_a, side, far_z, own_a), (1, pair_b, x, far_x, own_b)
+        ):
+            incoming(2 + kind, i, far.at[b])
+            total = pair[b, cols(mine * part, part)].astype(jnp.float32) + far[b].astype(jnp.float32)
+            full[b, own_cols] = (curv_ref[kind, b].astype(jnp.float32) * total).astype(jnp.bfloat16)
+            plans[i][4 + kind].start()
+
+    def widen(i):
+        b = block(i)
+        other_a, other_b = shard_columns(x, 1 - side, width)[0], shard_columns(1 - x, side, width)[1]
+        incoming(4, i, full.at[b, cols(other_a, part)])
+        plans[i][6].start()
+        incoming(5, i, full.at[b, cols(other_b, part)])
+        plans[i][7].start()
+
+    def finish(i):
+        b = block(i)
+        incoming(6, i, full.at[b, give_a])
+        incoming(7, i, full.at[b, give_b])
+        weighted_ref[b, :] = full[b, :]
+        back_ref[b, :] = lax.dot_general(
+            full[b, :], w_ref[...], (((1,), (1,)), ((), ())), preferred_element_type=jnp.float32
+        ).astype(jnp.bfloat16)
+
+    for i in range(chunks + 3):
+        if i < chunks:
+            terms_of(i)
+            plans[i][0].start()
+            plans[i][1].start()
+        if 0 <= i - 1 < chunks:
+            pair_up(i - 1)
+        if 0 <= i - 2 < chunks:
+            weigh(i - 2)
+        if 0 <= i - 3 < chunks:
+            widen(i - 3)
+    for i in range(chunks):
+        finish(i)
+    for plan in plans:
+        for one in plan:
+            one.wait_send()
+
+
+def square_exchange(mixed, d_mixed, w_out, p_out, curvature):
+    length, inner = mixed.shape
+    width = w_out.shape[1]
+    chunks = 4
+    vmem = pl.BlockSpec(memory_space=pltpu.VMEM)
+    quarter = pltpu.VMEM((length, width // 4), jnp.bfloat16)
+    part = pltpu.VMEM((length, width // 8), jnp.bfloat16)
+    whole = pltpu.VMEM((length, width), jnp.bfloat16)
+    return pl.pallas_call(
+        square_kernel,
+        out_shape=(
+            jax.ShapeDtypeStruct((length, width), jnp.bfloat16),
+            jax.ShapeDtypeStruct(mixed.shape, jnp.bfloat16),
+        ),
+        in_specs=[vmem] * 5,
+        out_specs=(vmem, vmem),
+        scratch_shapes=[
+            whole, quarter, quarter, quarter, quarter, part, part, whole,
+            pltpu.SemaphoreType.DMA((8, chunks)),
+            pltpu.SemaphoreType.DMA((8, chunks)),
+        ],
+        compiler_params=pltpu.CompilerParams(
+            collective_id=4, has_side_effects=True, vmem_limit_bytes=GRID_VMEM_BYTES
+        ),
+    )(mixed, d_mixed, w_out, p_out, curvature)
+
+
+def reduce_grid_kernel(n, slots, scale, grid_qkv, grid_out, pick_ref, normed_t_ref, d_proj_ref,
+                       mixed_t_ref, weighted_ref, out_ref, grads, peer, begin, across, onward,
+                       landed, core_send, core_recv, y_send, y_recv, z_send, z_recv):
+    planes = n // 2
+    z, y, x, c = spot()
+    zeta = mirrored(z, c, planes)
+    hub = lax.rem(zeta, 2) == 0
+    spoke = lax.rem(zeta, 2) == 1
+    late = lax.div(zeta, 2)
+    y_peer = device(z, 1 - y, x, c)
+    core_peer = device(z, y, x, 1 - c)
+    row = [device(lax.rem(z + i, planes), y, x, c) for i in range(1, planes)]
+    greet(row + [core_peer, y_peer])
+    cuts = cut_count(slots)
+    size = slots // cuts
+    rows, cols = grid_qkv
+    out_rows, out_cols = grid_out
+    total = rows * cols + out_rows * out_cols
+    edge = out_ref.shape[-1]
+    legs = core_send.shape[0] - 1
+    leg_rows = rows // legs
+    group = 2
+
+    def core_copy(i):
+        if i == legs:
+            here = pl.ds(rows * cols, out_rows * out_cols)
+        else:
+            here = pl.ds(i * leg_rows * cols, leg_rows * cols)
+        return pltpu.make_async_remote_copy(
+            src_ref=grads.at[here],
+            dst_ref=peer.at[here],
+            send_sem=core_send.at[i],
+            recv_sem=core_recv.at[i],
+            device_id=core_peer,
+            device_id_type=pl.DeviceIdType.MESH,
+        )
+
+    def out_columns(i, carry):
+        width = group * edge
+        right = weighted_ref[:, pl.ds(pl.multiple_of(i * width, width), width)]
+        block = jnp.dot(
+            mixed_t_ref[...], right, preferred_element_type=jnp.float32
+        ).astype(jnp.bfloat16)
+        for r in range(out_rows):
+            for k in range(group):
+                grads[rows * cols + r * out_cols + i * group + k] = block[
+                    r * edge:(r + 1) * edge, k * edge:(k + 1) * edge
+                ]
+        return carry
+
+    def qkv_rows(i, carry):
+        width = group * edge
+        left = normed_t_ref[pl.ds(pl.multiple_of(i * width, width), width), :]
+        block = jnp.dot(
+            left, d_proj_ref[...], preferred_element_type=jnp.float32
+        ).astype(jnp.bfloat16)
+        for r in range(group):
+            for k in range(cols):
+                grads[(i * group + r) * cols + k] = block[
+                    r * edge:(r + 1) * edge, k * edge:(k + 1) * edge
+                ]
+        return carry
+
+    def hand_over(i):
+        @pl.when(spoke)
+        def _():
+            core_copy(i).start()
+
+    grads[total] = jnp.zeros((edge, edge), grads.dtype)
+    peer[total] = jnp.zeros((edge, edge), peer.dtype)
+    lax.fori_loop(0, out_cols // group, out_columns, 0)
+    hand_over(legs)
+    for i in range(legs):
+        steps = leg_rows // group
+        lax.fori_loop(i * steps, (i + 1) * steps, qkv_rows, 0)
+        hand_over(i)
+
+    def owner(i, at_y):
+        first = (3, 2, 1, 0)[i]
+        second = (0, 1, 3, 2)[i]
+        o = (1 - late) * first + late * second
+        return 2 * mirrored(o, c, planes) + at_y
+
+    def both(index):
+        return grads[index].astype(jnp.float32) + peer[index].astype(jnp.float32)
+
+    def y_copy(i, j):
+        here = pl.ds(i * slots + j * size, size)
+        return pltpu.make_async_remote_copy(
+            src_ref=begin.at[here],
+            dst_ref=across.at[here],
+            send_sem=y_send.at[i, j],
+            recv_sem=y_recv.at[i, j],
+            device_id=y_peer,
+            device_id_type=pl.DeviceIdType.MESH,
+        )
+
+    def z_copy(i, j):
+        goal = (1 - late) * (2, 2, 1)[i] + late * (0, 1, 3)[i]
+        buffer = (0, 1, 0)[i]
+        return pltpu.make_async_remote_copy(
+            src_ref=onward.at[i, pl.ds(j * size, size)],
+            dst_ref=landed.at[buffer, pl.ds(j * size, size)],
+            send_sem=z_send.at[i, j],
+            recv_sem=z_recv.at[buffer, j],
+            device_id=device(mirrored(goal, c, planes), y, x, c),
+            device_id_type=pl.DeviceIdType.MESH,
+        )
+
+    def z_wait(buffer, j):
+        here = landed.at[buffer, pl.ds(j * size, size)]
+        pltpu.make_async_remote_copy(
+            src_ref=here,
+            dst_ref=here,
+            send_sem=z_send.at[0, j],
+            recv_sem=z_recv.at[buffer, j],
+            device_id=core_peer,
+            device_id_type=pl.DeviceIdType.MESH,
+        ).wait_recv()
+
+    def each(j, body):
+        def some(t, carry):
+            body(j * size + t)
+            return carry
+
+        lax.fori_loop(0, size, some, 0)
+
+    @pl.when(hub)
+    def _():
+        for i in (legs,) + tuple(range(legs)):
+            core_copy(i).wait_recv()
+        for i in range(planes):
+            base = owner(i, 1 - y) * slots
+
+            def start(j, carry, i=i, base=base):
+                def fill(t):
+                    begin[i * slots + t] = both(pick_ref[base + t]).astype(jnp.bfloat16)
+
+                each(j, fill)
+                y_copy(i, j).start()
+                return carry
+
+            lax.fori_loop(0, cuts, start, 0)
+        for i in range(planes):
+            base = owner(i, y) * slots
+
+            def value(t, i=i, base=base):
+                return both(pick_ref[base + t]) + across[i * slots + t].astype(jnp.float32)
+
+            def go(j, carry, i=i, value=value):
+                y_copy(i, j).wait_recv()
+                if i < 2:
+
+                    def pass_on(t):
+                        onward[i, t] = value(t).astype(jnp.bfloat16)
+
+                    each(j, pass_on)
+                    z_copy(i, j).start()
+                elif i == 2:
+
+                    @pl.when(late == 0)
+                    def _():
+                        def pass_on(t):
+                            onward[i, t] = value(t).astype(jnp.bfloat16)
+
+                        each(j, pass_on)
+
+                    @pl.when(late == 1)
+                    def _():
+                        z_wait(0, j)
+
+                        def pass_on(t):
+                            onward[i, t] = (
+                                value(t) + landed[0, t].astype(jnp.float32)
+                            ).astype(jnp.bfloat16)
+
+                        each(j, pass_on)
+
+                    z_copy(i, j).start()
+                else:
+                    z_wait(late, j)
+
+                    def last(t):
+                        out_ref[t] = (value(t) + landed[late, t].astype(jnp.float32)) * scale
+
+                    each(j, last)
+                return carry
+
+            lax.fori_loop(0, cuts, go, 0)
+
+        def close(j, carry):
+            for i in range(planes):
+                y_copy(i, j).wait_send()
+            for i in range(3):
+                z_copy(i, j).wait_send()
+            return carry
+
+        lax.fori_loop(0, cuts, close, 0)
+
+    @pl.when(spoke)
+    def _():
+        @pl.when(zeta == 1)
+        def _():
+            def go(j, carry):
+                z_wait(0, j)
+                z_wait(1, j)
+
+                def last(t):
+                    out_ref[t] = (
+                        landed[0, t].astype(jnp.float32) + landed[1, t].astype(jnp.float32)
+                    ) * scale
+
+                each(j, last)
+                return carry
+
+            lax.fori_loop(0, cuts, go, 0)
+
+        @pl.when(zeta == 3)
+        def _():
+            def go(j, carry):
+                z_wait(0, j)
+
+                def last(t):
+                    out_ref[t] = landed[0, t].astype(jnp.float32) * scale
+
+                each(j, last)
+                return carry
+
+            lax.fori_loop(0, cuts, go, 0)
+
+        for i in range(legs + 1):
+            core_copy(i).wait_send()
+
+
+def reduce_grid(picked, normed_t, d_proj, mixed_t, weighted, n, scale, grid_qkv, grid_out):
+    slots = picked.shape[0] // n
+    edge = BLK
+    total_blocks = grid_qkv[0] * grid_qkv[1] + grid_out[0] * grid_out[1]
+    cuts = cut_count(slots)
+    legs = 4
+    vmem = pl.BlockSpec(memory_space=pltpu.VMEM)
+    dma = pltpu.SemaphoreType.DMA
+    return pl.pallas_call(
+        functools.partial(reduce_grid_kernel, n, slots, scale, grid_qkv, grid_out),
+        out_shape=jax.ShapeDtypeStruct((slots, edge, edge), jnp.float32),
+        in_specs=[pl.BlockSpec(memory_space=pltpu.SMEM)] + [vmem] * 4,
+        out_specs=vmem,
+        scratch_shapes=[
+            pltpu.VMEM((total_blocks + 1, edge, edge), jnp.bfloat16),
+            pltpu.VMEM((total_blocks + 1, edge, edge), jnp.bfloat16),
+            pltpu.VMEM((n // 2 * slots, edge, edge), jnp.bfloat16),
+            pltpu.VMEM((n // 2 * slots, edge, edge), jnp.bfloat16),
+            pltpu.VMEM((3, slots, edge, edge), jnp.bfloat16),
+            pltpu.VMEM((2, slots, edge, edge), jnp.bfloat16),
+            dma((legs + 1,)),
+            dma((legs + 1,)),
+            dma((n // 2, cuts)),
+            dma((n // 2, cuts)),
+            dma((3, cuts)),
+            dma((2, cuts)),
+        ],
+        compiler_params=pltpu.CompilerParams(
+            collective_id=5, has_side_effects=True, vmem_limit_bytes=GRID_VMEM_BYTES
+        ),
+    )(picked, normed_t, d_proj, mixed_t, weighted)
+
+
+def local_grid(tokens, norm_gain, curvature, weight_slots, probe_slots, block_counts):
+    n_columns = lax.axis_size("seq")
+    n_owners = lax.axis_size("fsdp")
+    q_heads = HQ // n_columns
+    kv_heads = HK // n_columns
+    row_blocks = D // BLK
+    qkv_cols = (q_heads + 2 * kv_heads) * HD // BLK
+    out_rows = q_heads * HD // BLK
+    grid_qkv, grid_out = (row_blocks, qkv_cols), (out_rows, row_blocks)
+    total_blocks = row_blocks * qkv_cols + out_rows * row_blocks
+    slots = weight_slots.shape[1]
+    length = tokens.shape[1]
+    z, _, _, c = spot()
+    theirs = lax.ppermute(block_counts, "seq", [(i, i ^ 1) for i in range(n_columns)])
+    counts = jnp.where(lax.rem(z, 2) == c, block_counts, theirs)[0]
+    range_ends = jnp.cumsum(counts)
+    starts = range_ends - counts
+    owner_ids = jnp.arange(n_owners, dtype=jnp.int32)
+    block_ids = jnp.arange(total_blocks, dtype=jnp.int32)
+    owners = jnp.sum((range_ends[None, :] <= block_ids[:, None]).astype(jnp.int32), axis=1)
+    first_block = jnp.sum(
+        jnp.where(owners[:, None] == owner_ids[None, :], starts[None, :], 0), axis=1
+    )
+    slot_of = (owners * slots + block_ids - first_block).astype(jnp.int32)
+    projected, d_projected, w_out, p_out, normed_t, curv_part = gather_grid(
+        slot_of,
+        weight_slots[0],
+        probe_slots[0],
+        tokens[0],
+        norm_gain[None, :],
+        curvature[0],
+        n_owners,
+        grid_qkv,
+        grid_out,
+    )
+    cosine, sine = rotary(length, HD)
+
+    def inner(projected):
+        return attention(projected, cosine, sine, q_heads, kv_heads)
+
+    mixed, d_mixed = jax.jvp(inner, (projected,), (d_projected,))
+    weighted, back_mixed = square_exchange(mixed, d_mixed, w_out, p_out, curv_part)
+    mixed_again, pullback = jax.vjp(inner, projected)
+    (back_projected,) = pullback(back_mixed)
+    slot_index = jnp.arange(n_owners * slots, dtype=jnp.int32)
+    place = slot_index % slots
+    owner_hot = (slot_index // slots)[:, None] == owner_ids[None, :]
+    owner_first = jnp.sum(jnp.where(owner_hot, starts[None, :], 0), axis=1)
+    own_count = jnp.sum(jnp.where(owner_hot, counts[None, :], 0), axis=1)
+    picked = jnp.where(place < own_count, owner_first + place, total_blocks).astype(jnp.int32)
+    scaled = reduce_grid(
+        picked,
+        normed_t,
+        back_projected.astype(jnp.bfloat16),
+        mixed_again.T,
+        weighted,
+        n_owners,
+        (length * n_owners) ** -0.5,
+        grid_qkv,
+        grid_out,
+    )
+    return scaled.reshape(1, slots, BLK, BLK)
+
+
 def solution(mesh):
     in_specs = (
         P("fsdp", None, None),
@@ -590,4 +1436,5 @@
         P("seq", None),
     )
     out_specs = P("seq", "fsdp", None, None)
-    return jax.shard_map(local, mesh=mesh, in_specs=in_specs, out_specs=out_specs, check_vma=False)
+    body = local_grid if mesh.shape["fsdp"] == 8 and mesh.shape["seq"] == 4 else local
+    return jax.shard_map(body, mesh=mesh, in_specs=in_specs, out_specs=out_specs, check_vma=False)

time: 521 us -> 417 us (0.80)
  Pallas kernels: 475 us -> 369 us
    pallas_call x3, Pallas kernels: 475 us -> 369 us  [the longest x1 181 us: gather_grid(): pl.pallas_call(functools.partial(gather_grid_kernel, n, slots, grid_qkv,...]
  transfers between devices with their start and end apart: 0 -> 1, of which waited for: 0 -> 0; matrix products, arithmetic and copies ran while one was open for 0% -> 1% of each run, Pallas kernels for 0% -> 0%
where the time goes in v1:
time: 417 us
  Pallas kernels  369 us (88%)
  matrix products  20.4 us (5%)
  local copies, waits for them, and re-layouts  14.1 us (3%)
  other arithmetic  12.9 us (3%)
    pallas_call x1, Pallas kernels, gather_grid(): pl.pallas_call(functools.partial(gather_grid_kernel, n, slots, grid_qkv,...  181 us
    pallas_call x1, Pallas kernels, reduce_grid(): pl.pallas_call(functools.partial(reduce_grid_kernel, n, slots, scale, gri...  108 us
    pallas_call x1, Pallas kernels, square_exchange(): pl.pallas_call(square_kernel, out_shape=(jax.ShapeDtypeStruct((length, wi...  80.1 us
    dot_general x5, matrix products, attention(): jnp.einsum('kgqs,skd->qkgd', attn_probs, values, preferred_element_type=j...  12.1 us
    dot_general x5, matrix products, attention(): jnp.einsum('qkgd,skd->kgqs', queries, key_rows, preferred_element_type=jn...  8.35 us
  transfers between devices with their start and end apart: 1, of which 0 were waited for; matrix products, arithmetic and copies ran while one was open for 1% of the time, Pallas kernels for 0%

profile of v1, /device:TPU:1, one launch (start us, length us, event | category | flops | bytes accessed | tf_op | source)
XLA Modules:
  0.0 416.9 jit_solution(2688704806642172526)
XLA Ops:
  0.0 0.0 collective-permute-start
  0.0 0.8 iota_compare_fusion
  0.8 0.6 add_select_fusion
  1.4 1.7 fusion.57
  3.1 0.0 collective-permute-done
  3.2 0.0 copy-start.29
  3.2 0.2 reduce-window.4
  3.4 0.1 convert_reduce_fusion
  3.4 0.1 select_reduce_fusion.2
  3.5 0.6 add_subtract_fusion.slot_ref
  4.1 0.0 copy-done.24
  4.1 0.0 copy-done.29
  4.1 180.9 %shard_map.64 = (f32[512,768]{1,0:T(8,128)}, f32[512,768]{1,0:T(8,128)}, bf16[512,4096]{1,0:T(8,128)(2,1)}, bf16[512,4096]{1,0:T(8,128)(2,1)}, bf16[4096,512]{1,0:T(8,128)(2,1)}, /*index=5*/bf16[2,512,512]{2,1,0:T(8,128)(2,1)}) custom-call(s32[320]{0:T(512)} %add_subtract_fusion.slot_ref, bf16[50,128,128]{2,1,0:T(8,128)(2,1)} %bitcast.204, ...), custom_call_target="tpu_custom_call" | custom-call | tf_op jit(solution)/shard_map/pallas_call | solution.py:923
  185.0 1.3 slice.55
  186.3 1.8 slice_bitcast_fusion
  188.1 1.3 slice.62
  189.4 0.4 reshape.292
  189.8 0.4 reshape.295
  190.1 2.4 fusion.68
  192.6 1.2 fusion.88
  193.8 0.5 subtract_convert_fusion
  194.4 0.3 copy-done.3
  194.7 1.2 fusion.10
  195.9 0.9 fusion.87
  196.9 1.0 divide_convert_fusion
  197.9 0.0 copy-start.2
  197.9 0.8 fusion.63
  198.7 2.1 fusion.90
  200.8 1.4 fusion.26
  202.3 2.9 fusion.11
  205.2 1.4 fusion.22
  206.6 1.0 copy.62.d_mixed_ref
  207.6 1.1 copy.38.mixed_ref
  208.7 80.1 %shard_map.65 = (bf16[512,4096]{1,0:T(8,128)(2,1)}, bf16[512,512]{1,0:T(8,128)(2,1)}) custom-call(bf16[512,512]{1,0:T(8,128)(2,1)} %copy.38.mixed_ref, bf16[512,512]{1,0:T(8,128)(2,1)} %copy.62.d_mixed_ref, bf16[512,4096]{1,0:T(8,128)(2,1)} %get-tuple-element.16.w_ref, bf16[512,4096]{1,0:T(8,128)(2,1)} %get-tuple-element.17.p_ref, ...), custom_call_target="tpu_custom_call" | custom-call | tf_op jit(solution)/shard_map/pallas_call | solution.py:1079
  288.8 1.3 copy.63
  290.0 2.3 fusion.44
  292.4 4.0 fusion.8
  296.5 2.2 fusion.50
  298.8 2.1 fusion.25
  300.9 1.4 multiply_add_fusion.3
  302.3 0.5 multiply_add_fusion.1
  302.8 0.1 add_bitcast_fusion.1
  303.0 0.3 copy_bitcast_fusion
  303.3 0.1 select_reduce_fusion.1
  303.4 0.6 add_select_fusion.2.pick_ref
  304.0 1.0 add_convert_fusion.2.d_proj_ref
  305.0 107.9 %shard_map.66 = f32[50,128,128]{2,1,0:T(8,128)} custom-call(s32[400]{0:T(512)} %add_select_fusion.2.pick_ref, bf16[4096,512]{1,0:T(8,128)(2,1)} %get-tuple-element.13.normed_t_ref, bf16[512,768]{1,0:T(8,128)(2,1)} %add_convert_fusion.2.d_proj_ref, bf16[512,512]{1,0:T(8,128)(2,1)} %bitcast.198, bf16[512,4096]{1,0:T(8,128)(2,1)} %get-tuple-element.20.weighted_ref), custom_call_target="tpu_custom_call" | custom-call | tf_op jit(solution)/shard_map/pallas_call | solution.py:1340
  412.9 4.0 copy.82
  (63 shorter events, 0.2 us)
Async XLA Ops:
  0.0 3.1 collective-permute-start
  0.0 4.1 copy-start.24
  3.2 1.0 copy-start.29
  3.4 0.8 copy-start.27
  186.3 3.8 copy-start.25
  192.5 6.1 %copy-start.14 = (bf16[512,64]{1,0:T(8,128)(2,1)}, bf16[512,64]{1,0:T(8,128)(2,1)S(1)}, u32[]{:S(2)}) copy-start(bf16[512,64]{1,0:T(8,128)(2,1)S(1)} %get-tuple-element.41) | copy-start | bytes 196612
  192.6 6.1 %copy-start.16 = (bf16[512,64]{1,0:T(8,128)(2,1)}, bf16[512,64]{1,0:T(8,128)(2,1)S(1)}, u32[]{:S(2)}) copy-start(bf16[512,64]{1,0:T(8,128)(2,1)S(1)} %get-tuple-element.42) | copy-start | bytes 196612
  192.6 1.2 copy-start.10
  192.6 1.2 copy-start.12
  193.8 1.0 copy-start.3
  194.4 3.5 copy-start.6
  194.4 3.5 copy-start.8
  195.9 6.3 %copy-start = (f32[512,512,4]{1,0,2:T(8,128)}, f32[512,512,4]{1,0,2:T(8,128)S(1)}, u32[]{:S(2)}) copy-start(f32[512,512,4]{1,0,2:T(8,128)S(1)} %get-tuple-element.46) | copy-start | bytes 12582916
  195.9 6.3 %copy-start.18 = (f32[4,512]{1,0:T(4,128)}, f32[4,512]{1,0:T(4,128)S(1)}, u32[]{:S(2)}) copy-start(f32[4,512]{1,0:T(4,128)S(1)} %get-tuple-element.45) | copy-start | bytes 24580
  196.8 5.4 %copy-start.20 = (f32[4,512]{1,0:T(4,128)}, f32[4,512]{1,0:T(4,128)S(1)}, u32[]{:S(2)}) copy-start(f32[4,512]{1,0:T(4,128)S(1)} %fusion.87) | copy-start | bytes 24580
  196.9 5.4 %copy-start.23 = (f32[4,512]{1,0:T(4,128)}, f32[4,512]{1,0:T(4,128)S(1)}, u32[]{:S(2)}) copy-start(f32[4,512]{1,0:T(4,128)S(1)} %multiply_divide_fusion) | copy-start | bytes 24580
  197.9 7.3 %copy-start.2 = (bf16[1,4,512,512]{2,3,1,0:T(8,128)(2,1)}, bf16[1,4,512,512]{2,3,1,0:T(8,128)(2,1)S(1)}, u32[]{:S(2)}) copy-start(bf16[1,4,512,512]{2,3,1,0:T(8,128)(2,1)S(1)} %divide_convert_fusion) | copy-start | bytes 6291460
  202.2 5.4 %copy-start.5 = (bf16[128,4,512]{2,0,1:T(8,128)(2,1)}, bf16[128,4,512]{2,0,1:T(8,128)(2,1)S(1)}, u32[]{:S(2)}) copy-start(bf16[128,4,512]{2,0,1:T(8,128)(2,1)S(1)} %fusion.26) | copy-start | bytes 1572868
  292.3 4.1 copy-start.1
  292.3 4.1 copy-start.4
  292.4 4.1 copy-start.7
  292.4 4.1 copy-start.9
  292.4 4.1 copy-start.19
  292.4 4.1 copy-start.21
  296.5 2.2 copy-start.15
  296.5 2.2 copy-start.17
  298.7 2.2 copy-start.26
  298.7 3.6 copy-start.11
  298.8 3.6 copy-start.13
  302.3 1.0 copy-start.22
  302.3 1.0 copy-start.28
  302.3 1.0 copy-start.30

commit v2 on v1

--- a/solution.py
+++ b/solution.py
@@ -949,13 +949,145 @@
     )(slot_of, weights, probes, tokens, gain, curvature)
 
 
-def square_kernel(mixed_ref, d_mixed_ref, w_ref, p_ref, curv_ref, weighted_ref, back_ref, terms,
-                  near_x, near_z, pair_a, pair_b, far_z, far_x, full, send_sem, recv_sem):
+def turn_tables(length, head_dim):
+    cosine, sine = rotary(length, head_dim)
+    cosine, sine = cosine[:, 0, :], sine[:, 0, :]
+    return jnp.concatenate([cosine, cosine], axis=1), jnp.concatenate([-sine, sine], axis=1)
+
+
+def turn(values, cosine, sine):
+    return values * cosine + pltpu.roll(values, values.shape[1] // 2, 1) * sine
+
+
+def attend(heads, proj_ref, d_proj_ref, cos_ref, sin_ref, mixed_ref, d_mixed_ref, mixed_t_ref,
+           probs_ref, rot_ref, d_rot):
+    length = proj_ref.shape[0]
+    hd = cos_ref.shape[1]
+    key_at = heads * hd
+    val_at = key_at + hd
+    scale = hd ** -0.5
+
+    def spin(source, target):
+        def some(h, carry):
+            here = pl.ds(pl.multiple_of(h * hd, hd), hd)
+            target[:, here] = turn(source[:, here], cos_ref[...], sin_ref[...]).astype(jnp.bfloat16)
+            return carry
+
+        lax.fori_loop(0, heads + 1, some, 0)
+        target[:, val_at:] = source[:, val_at:].astype(jnp.bfloat16)
+
+    spin(proj_ref, rot_ref)
+    spin(d_proj_ref, d_rot)
+    tile = hd
+
+    def head(h, carry):
+        here = pl.ds(pl.multiple_of(h * hd, hd), hd)
+        for i in range(length // tile):
+            rows = slice(i * tile, (i + 1) * tile)
+            span = (i + 1) * tile
+            q, dq = rot_ref[rows, here], d_rot[rows, here]
+            k, dk = rot_ref[:span, key_at:val_at], d_rot[:span, key_at:val_at]
+            v, dv = rot_ref[:span, val_at:], d_rot[:span, val_at:]
+            contract = (((1,), (1,)), ((), ()))
+            scores = lax.dot_general(q, k, contract, preferred_element_type=jnp.float32) * scale
+            slopes = lax.dot_general(
+                jnp.concatenate([dq, q], axis=1),
+                jnp.concatenate([k, dk], axis=1),
+                contract,
+                preferred_element_type=jnp.float32,
+            ) * scale
+            at_row = i * tile + lax.broadcasted_iota(jnp.int32, (tile, span), 0)
+            at_col = lax.broadcasted_iota(jnp.int32, (tile, span), 1)
+            seen = at_row >= at_col
+            scores = jnp.where(seen, scores, NEGATIVE)
+            slopes = jnp.where(seen, slopes, 0.0)
+            raised = jnp.exp(scores - jnp.max(scores, axis=1, keepdims=True))
+            probs = raised / jnp.sum(raised, axis=1, keepdims=True)
+            d_probs = probs * (slopes - jnp.sum(probs * slopes, axis=1, keepdims=True))
+            probs = probs.astype(jnp.bfloat16)
+            d_probs = d_probs.astype(jnp.bfloat16)
+            probs_ref[h, rows, :span] = probs
+            if span < length:
+                probs_ref[h, rows, span:] = jnp.zeros((tile, length - span), jnp.bfloat16)
+            mixed = jnp.dot(probs, v, preferred_element_type=jnp.float32).astype(jnp.bfloat16)
+            mixed_ref[rows, here] = mixed
+            mixed_t_ref[here, rows] = mixed.T
+            d_mixed_ref[rows, here] = (
+                jnp.dot(d_probs, v, preferred_element_type=jnp.float32)
+                + jnp.dot(probs, dv, preferred_element_type=jnp.float32)
+            ).astype(jnp.bfloat16)
+        return carry
+
+    lax.fori_loop(0, heads, head, 0)
+
+
+def attend_back(heads, back_ref, probs_ref, rot_ref, cos_ref, sin_ref, out_ref, slope_ref):
+    length = back_ref.shape[0]
+    hd = cos_ref.shape[1]
+    key_at = heads * hd
+    val_at = key_at + hd
+    scale = hd ** -0.5
+    tile = hd
+
+    def unturn(values):
+        rounded = values.astype(jnp.bfloat16).astype(jnp.float32)
+        return turn(rounded, cos_ref[...], -sin_ref[...]).astype(jnp.bfloat16)
+
+    def head(h, totals):
+        here = pl.ds(pl.multiple_of(h * hd, hd), hd)
+        key_total, val_total = totals
+        for i in range(length // tile):
+            rows = slice(i * tile, (i + 1) * tile)
+            span = (i + 1) * tile
+            back = back_ref[rows, here]
+            d_probs = lax.dot_general(
+                back, rot_ref[:span, val_at:], (((1,), (1,)), ((), ())),
+                preferred_element_type=jnp.float32,
+            ).astype(jnp.bfloat16).astype(jnp.float32)
+            probs = probs_ref[h, rows, :span].astype(jnp.float32)
+            slopes = probs * (d_probs - jnp.sum(probs * d_probs, axis=1, keepdims=True)) * scale
+            slope_ref[rows, :span] = slopes.astype(jnp.bfloat16)
+            if span < length:
+                slope_ref[rows, span:] = jnp.zeros((tile, length - span), jnp.bfloat16)
+        slopes = slope_ref[...]
+        d_query = jnp.dot(slopes, rot_ref[:, key_at:val_at], preferred_element_type=jnp.float32)
+        out_ref[:, here] = unturn(d_query)
+        first = (((0,), (0,)), ((), ()))
+        key_total = key_total + lax.dot_general(
+            rot_ref[:, here], slopes, first, preferred_element_type=jnp.float32
+        )
+        val_total = val_total + lax.dot_general(
+            back_ref[:, here], probs_ref[h], first, preferred_element_type=jnp.float32
+        )
+        return key_total, val_total
+
+    zero = jnp.zeros((hd, length), jnp.float32)
+    key_total, val_total = lax.fori_loop(0, heads, head, (zero, zero))
+    out_ref[:, key_at:val_at] = unturn(key_total.T)
+    out_ref[:, val_at:] = val_total.T.astype(jnp.bfloat16)
+
+
+def square_kernel(heads, proj_ref, d_proj_ref, w_out, p_out, curv_ref, cos_ref, sin_ref,
+                  weighted_ref, back_proj_ref, mixed_t_ref, w_ref, p_ref, mixed_ref, d_mixed_ref,
+                  probs, rot, d_rot, slope, back_ref, terms, near_x, near_z, pair_a, pair_b, far_z,
+                  far_x, full, load_sem, send_sem, recv_sem):
     z, y, x, c = spot()
     side = lax.rem(z, 2)
     x_peer = device(z, y, 1 - x, c)
     z_peer = device(z + 1 - 2 * side, y, x, c)
+    loads = [
+        pltpu.make_async_copy(w_out, w_ref, load_sem.at[0]),
+        pltpu.make_async_copy(p_out, p_ref, load_sem.at[1]),
+    ]
+    for load in loads:
+        load.start()
     greet([x_peer, z_peer])
+    attend(
+        heads, proj_ref, d_proj_ref, cos_ref, sin_ref, mixed_ref, d_mixed_ref, mixed_t_ref, probs,
+        rot, d_rot,
+    )
+    for load in loads:
+        load.wait()
     length, width = terms.shape
     quarter, part = width // 4, width // 8
     chunks = recv_sem.shape[1]
@@ -1063,36 +1195,51 @@
             widen(i - 3)
     for i in range(chunks):
         finish(i)
+    attend_back(heads, back_ref, probs, rot, cos_ref, sin_ref, back_proj_ref, slope)
     for plan in plans:
         for one in plan:
             one.wait_send()
 
 
-def square_exchange(mixed, d_mixed, w_out, p_out, curvature):
-    length, inner = mixed.shape
-    width = w_out.shape[1]
+def square_exchange(projected, d_projected, w_out, p_out, curvature, cosine, sine, heads):
+    length, inputs = projected.shape
+    inner, width = w_out.shape
     chunks = 4
+    half = jnp.bfloat16
     vmem = pl.BlockSpec(memory_space=pltpu.VMEM)
-    quarter = pltpu.VMEM((length, width // 4), jnp.bfloat16)
-    part = pltpu.VMEM((length, width // 8), jnp.bfloat16)
-    whole = pltpu.VMEM((length, width), jnp.bfloat16)
+    anywhere = pl.BlockSpec(memory_space=pl.ANY)
+    quarter = pltpu.VMEM((length, width // 4), half)
+    part = pltpu.VMEM((length, width // 8), half)
+    whole = pltpu.VMEM((length, width), half)
+    narrow = pltpu.VMEM((length, inner), half)
     return pl.pallas_call(
-        square_kernel,
+        functools.partial(square_kernel, heads),
         out_shape=(
-            jax.ShapeDtypeStruct((length, width), jnp.bfloat16),
-            jax.ShapeDtypeStruct(mixed.shape, jnp.bfloat16),
+            jax.ShapeDtypeStruct((length, width), half),
+            jax.ShapeDtypeStruct((length, inputs), half),
+            jax.ShapeDtypeStruct((inner, length), half),
         ),
-        in_specs=[vmem] * 5,
-        out_specs=(vmem, vmem),
+        in_specs=[vmem] * 2 + [anywhere] * 2 + [vmem] * 3,
+        out_specs=(vmem,) * 3,
         scratch_shapes=[
+            pltpu.VMEM((inner, width), half),
+            pltpu.VMEM((inner, width), half),
+            narrow,
+            narrow,
+            pltpu.VMEM((heads, length, length), half),
+            pltpu.VMEM((length, inputs), half),
+            pltpu.VMEM((length, inputs), half),
+            pltpu.VMEM((length, length), half),
+            narrow,
             whole, quarter, quarter, quarter, quarter, part, part, whole,
+            pltpu.SemaphoreType.DMA((2,)),
             pltpu.SemaphoreType.DMA((8, chunks)),
             pltpu.SemaphoreType.DMA((8, chunks)),
         ],
         compiler_params=pltpu.CompilerParams(
             collective_id=4, has_side_effects=True, vmem_limit_bytes=GRID_VMEM_BYTES
         ),
-    )(mixed, d_mixed, w_out, p_out, curvature)
+    )(projected, d_projected, w_out, p_out, curvature, cosine, sine)
 
 
 def reduce_grid_kernel(n, slots, scale, grid_qkv, grid_out, pick_ref, normed_t_ref, d_proj_ref,
@@ -1397,15 +1544,10 @@
         grid_qkv,
         grid_out,
     )
-    cosine, sine = rotary(length, HD)
-
-    def inner(projected):
-        return attention(projected, cosine, sine, q_heads, kv_heads)
-
-    mixed, d_mixed = jax.jvp(inner, (projected,), (d_projected,))
-    weighted, back_mixed = square_exchange(mixed, d_mixed, w_out, p_out, curv_part)
-    mixed_again, pullback = jax.vjp(inner, projected)
-    (back_projected,) = pullback(back_mixed)
+    cosine, sine = turn_tables(length, HD)
+    weighted, back_projected, mixed_t = square_exchange(
+        projected, d_projected, w_out, p_out, curv_part, cosine, sine, q_heads
+    )
     slot_index = jnp.arange(n_owners * slots, dtype=jnp.int32)
     place = slot_index % slots
     owner_hot = (slot_index // slots)[:, None] == owner_ids[None, :]
@@ -1415,8 +1557,8 @@
     scaled = reduce_grid(
         picked,
         normed_t,
-        back_projected.astype(jnp.bfloat16),
-        mixed_again.T,
+        back_projected,
+        mixed_t,
         weighted,
         n_owners,
         (length * n_owners) ** -0.5,

time: 417 us -> 387 us (0.928)
  matrix products: 20.4 us -> 0 us
  local copies, waits for them, and re-layouts: 14.1 us -> 4.01 us
  Pallas kernels: 369 us -> 379 us
  other arithmetic: 12.9 us -> 3.65 us
    dot_general x10 -> x0, matrix products: 20.4 us -> none  [the longest x5 12.1 us: attention(): jnp.einsum('kgqs,skd->qkgd', attn_probs, values, preferred_element_type=j...]
    pallas_call x1, Pallas kernels: 80.1 us -> 89.6 us  [square_exchange(): pl.pallas_call(functools.partial(square_kernel, heads), out_shape=(jax.Sh...]
where the time goes in v2:
time: 387 us; the launch traced here: 386 us
  Pallas kernels  379 us (98%)
  local copies, waits for them, and re-layouts  4.01 us (1%)
    pallas_call x1, Pallas kernels, gather_grid(): pl.pallas_call(functools.partial(gather_grid_kernel, n, slots, grid_qkv,...  181 us
    pallas_call x1, Pallas kernels, reduce_grid(): pl.pallas_call(functools.partial(reduce_grid_kernel, n, slots, scale, gri...  108 us
    pallas_call x1, Pallas kernels, square_exchange(): pl.pallas_call(functools.partial(square_kernel, heads), out_shape=(jax.Sh...  89.6 us
  transfers between devices with their start and end apart: 1, of which 0 were waited for; matrix products, arithmetic and copies ran while one was open for 1% of the time, Pallas kernels for 0%

profile of v2, /device:TPU:1, one launch (start us, length us, event | category | flops | bytes accessed | tf_op | source)
XLA Modules:
  0.0 386.4 jit_solution(12938231502615926091)
XLA Ops:
  0.0 0.0 collective-permute-start
  0.0 1.0 fusion.2
  1.0 1.0 pad_maximum_fusion
  2.1 0.0 collective-permute-done
  2.1 0.2 reduce-window.4
  2.3 0.1 convert_reduce_fusion
  2.3 0.1 select_reduce_fusion.2
  2.4 0.6 add_subtract_fusion.slot_ref
  3.0 0.1 select_reduce_fusion.1
  3.1 0.6 add_select_fusion.2.pick_ref
  3.7 181.0 %shard_map.64 = (f32[512,768]{1,0:T(8,128)}, f32[512,768]{1,0:T(8,128)}, bf16[512,4096]{1,0:T(8,128)(2,1)}, bf16[512,4096]{1,0:T(8,128)(2,1)}, bf16[4096,512]{1,0:T(8,128)(2,1)}, /*index=5*/bf16[2,512,512]{2,1,0:T(8,128)(2,1)}) custom-call(s32[320]{0:T(512)} %add_subtract_fusion.slot_ref, bf16[50,128,128]{2,1,0:T(8,128)(2,1)} %bitcast.18, ...), custom_call_target="tpu_custom_call" | custom-call | tf_op jit(solution)/shard_map/pallas_call | solution.py:923
  184.8 89.6 %shard_map.65 = (bf16[512,4096]{1,0:T(8,128)(2,1)}, bf16[512,768]{1,0:T(8,128)(2,1)}, bf16[512,512]{1,0:T(8,128)(2,1)}) custom-call(f32[512,768]{1,0:T(8,128)} %get-tuple-element.15.proj_ref, f32[512,768]{1,0:T(8,128)} %get-tuple-element.16.d_proj_ref, bf16[512,4096]{1,0:T(8,128)(2,1)} %get-tuple-element.17.w_out, ...), custom_call_target="tpu_custom_call" | custom-call | tf_op jit(solution)/shard_map/pallas_call | solution.py:1215
  274.3 108.0 %shard_map.66 = f32[50,128,128]{2,1,0:T(8,128)} custom-call(s32[400]{0:T(512)} %add_select_fusion.2.pick_ref, bf16[4096,512]{1,0:T(8,128)(2,1)} %get-tuple-element.14.normed_t_ref, bf16[512,768]{1,0:T(8,128)(2,1)} %get-tuple-element.20.d_proj_ref, bf16[512,512]{1,0:T(8,128)(2,1)} %get-tuple-element.21.mixed_t_ref, ...), custom_call_target="tpu_custom_call" | custom-call | tf_op jit(solution)/shard_map/pallas_call | solution.py:1487
  382.4 4.0 %copy.8 = f32[1,50,128,128]{3,2,1,0:T(8,128)} copy(f32[1,50,128,128]{3,2,1,0:T(8,128)} %bitcast.15) | data formatting | bytes 6553600
  (4 shorter events, 0.0 us)
Async XLA Ops:
  0.0 2.1 collective-permute-start

commit v3 on v2

--- a/solution.py
+++ b/solution.py
@@ -611,8 +611,9 @@
 
 
 def gather_grid_kernel(n, slots, grid_qkv, grid_out, slot_ref, w_ref, p_ref, tokens_ref, gain_ref,
-                       curv_ref, proj_ref, d_proj_ref, wo_ref, po_ref, normed_t_ref, curv_out_ref,
-                       held_w, held_p, matrix, normed, curv_part, send_y, send_core, send_z, recv, tok_send,
+                       curv_ref, proj_out, d_proj_ref, wo_out, po_out, normed_t_out, curv_out,
+                       held_w, held_p, matrix, normed, wo_ref, po_ref, normed_t_ref, proj_ref,
+                       curv_part, in_sem, out_sem, send_y, send_core, send_z, recv, tok_send,
                        tok_recv, relay_send, relay_recv, curv_send, curv_recv):
     planes = n // 2
     z, y, x, c = spot()
@@ -625,12 +626,34 @@
     core_peer = device(z, y, x, 1 - c)
     z_peer = device(mate, y, x, c)
     row = [device(lax.rem(z + i, planes), y, x, c) for i in range(1, planes)]
-    greet(row + [core_peer, y_peer, x_peer])
     cuts = cut_count(slots)
     size = slots // cuts
     own = (w_ref, p_ref)
     held = (held_w, held_p)
     me = 2 * z + y
+
+    def own_load(which):
+        here = held[which].at[pl.ds(me * slots, slots)]
+        return pltpu.make_async_copy(own[which], here, in_sem.at[which])
+
+    def token_load():
+        return pltpu.make_async_copy(tokens_ref, normed, in_sem.at[2])
+
+    stores = [
+        pltpu.make_async_copy(here, there, out_sem.at[i])
+        for i, (here, there) in enumerate((
+            (normed_t_ref, normed_t_out), (proj_ref, proj_out), (wo_ref, wo_out),
+            (po_ref, po_out), (curv_part, curv_out),
+        ))
+    ]
+
+    @pl.when(hub)
+    def _():
+        token_load().start()
+        for which in range(2):
+            own_load(which).start()
+
+    greet(row + [core_peer, y_peer, x_peer])
     tok_cuts = tok_send.shape[0]
     half = normed.shape[0] // 2
     tok_rows = half // tok_cuts
@@ -713,20 +736,18 @@
             move(src, which, me, j, end_hub, send_z.at[1, k]),
         )
 
-    lead = min(2, 2 * cuts)
+    lead = min(6, 2 * cuts)
     every = [(which, j) for which in range(2) for j in range(cuts)]
 
     @pl.when(hub)
     def _():
         for k in range(lead):
             to_y(*every[k]).start()
-        for k, one in enumerate(every):
-            to_z(*one).start()
+        for k in range(max(len(every), tok_cuts)):
+            if k < len(every):
+                to_z(*every[k]).start()
             if k < tok_cuts:
                 token_copy(k, x, z_peer, tok_send, tok_recv, tokens_ref).start()
-            to_core(*one).start()
-        for k in range(len(every), tok_cuts):
-            token_copy(k, x, z_peer, tok_send, tok_recv, tokens_ref).start()
         for i in range(2):
             curv_copy(i).start()
             curv_local(i).start()
@@ -739,6 +760,7 @@
 
     def pass_row(k):
         which, j = every[k]
+        to_core(which, j).start()
         for r in range(1, planes):
             d = 2 * at(lax.rem(zeta + r, planes)) + y
             arrive(which, d, j)
@@ -773,12 +795,12 @@
             for d in range(n):
                 arrive(which, d, j)
 
-    def normalize(source):
+    def normalize():
         rows = 32
 
         def some(i, carry):
             here = pl.ds(pl.multiple_of(i * rows, rows), rows)
-            values = source[here, :].astype(jnp.float32)
+            values = normed[here, :].astype(jnp.float32)
             factor = lax.rsqrt(jnp.mean(values * values, axis=-1, keepdims=True) + EPS)
             normed[here, :] = (values * factor * gain_ref[...]).astype(jnp.bfloat16)
             return carry
@@ -837,11 +859,11 @@
     def keep_own(which):
         @pl.when(hub)
         def _():
-            held[which][pl.ds(me * slots, slots)] = own[which][...]
+            own_load(which).wait()
 
     @pl.when(hub)
     def _():
-        normalize(tokens_ref)
+        token_load().wait()
 
     @pl.when(spoke)
     def _():
@@ -852,18 +874,23 @@
             token_copy(i, 1 - x, x_peer, relay_send, relay_recv, normed).wait_recv()
         for i in range(tok_cuts):
             token_copy(i, x, x_peer, relay_send, relay_recv, normed).wait_send()
-        normalize(normed)
-
+
+    normalize()
     for j in range(cuts):
         step(0, j)
         if j == 0:
             transpose()
+            stores[0].start()
     keep_own(0)
-    todo = [
-        lambda: unpack_qkv(0),
-        lambda: project(proj_ref),
-        lambda: unpack_out(0, wo_ref),
-    ]
+    def first_proj():
+        project(proj_ref)
+        stores[1].start()
+
+    def first_out():
+        unpack_out(0, wo_ref)
+        stores[2].start()
+
+    todo = [lambda: unpack_qkv(0), first_proj, first_out]
     for j in range(cuts):
         step(1, j)
         if j < cuts - 1 and todo:
@@ -871,9 +898,8 @@
     while todo:
         todo.pop(0)()
     keep_own(1)
-    unpack_qkv(1)
-    project(d_proj_ref)
     unpack_out(1, po_ref)
+    stores[3].start()
 
     @pl.when(hub)
     def _():
@@ -885,7 +911,9 @@
         for i in range(2):
             curv_copy(i).wait_recv()
 
-    curv_out_ref[...] = curv_part[...]
+    stores[4].start()
+    unpack_qkv(1)
+    project(d_proj_ref)
 
     @pl.when(hub)
     def _():
@@ -909,6 +937,9 @@
             for copy in spoke_own(*one):
                 copy.wait_send()
 
+    for store in stores:
+        store.wait()
+
 
 def gather_grid(slot_of, weights, probes, tokens, gain, curvature, n, grid_qkv, grid_out):
     slots, edge, _ = weights.shape
@@ -919,19 +950,25 @@
     out = jax.ShapeDtypeStruct((grid_out[0] * edge, grid_out[1] * edge), jnp.bfloat16)
     shard = (2, length, width // 8)
     vmem = pl.BlockSpec(memory_space=pltpu.VMEM)
+    anywhere = pl.BlockSpec(memory_space=pl.ANY)
     dma = pltpu.SemaphoreType.DMA
     return pl.pallas_call(
         functools.partial(gather_grid_kernel, n, slots, grid_qkv, grid_out),
         out_shape=(proj, proj, out, out, turned, jax.ShapeDtypeStruct(shard, jnp.bfloat16)),
-        in_specs=[pl.BlockSpec(memory_space=pltpu.SMEM)] + [vmem] * 4
-        + [pl.BlockSpec(memory_space=pl.ANY)],
-        out_specs=(vmem,) * 6,
+        in_specs=[pl.BlockSpec(memory_space=pltpu.SMEM)] + [anywhere] * 3 + [vmem, anywhere],
+        out_specs=(anywhere, vmem) + (anywhere,) * 4,
         scratch_shapes=[
             pltpu.VMEM((n * slots, edge, edge), jnp.bfloat16),
             pltpu.VMEM((n * slots, edge, edge), jnp.bfloat16),
             pltpu.VMEM((grid_qkv[0] * edge, grid_qkv[1] * edge), jnp.bfloat16),
             pltpu.VMEM((length, width), jnp.bfloat16),
+            pltpu.VMEM(out.shape, out.dtype),
+            pltpu.VMEM(out.shape, out.dtype),
+            pltpu.VMEM(turned.shape, turned.dtype),
+            pltpu.VMEM(proj.shape, proj.dtype),
             pltpu.VMEM(shard, jnp.bfloat16),
+            dma((3,)),
+            dma((5,)),
             dma((n // 2, 2 * cuts)),
             dma((n, 2 * cuts)),
             dma((2, 2 * cuts)),
@@ -1068,9 +1105,9 @@
 
 
 def square_kernel(heads, proj_ref, d_proj_ref, w_out, p_out, curv_ref, cos_ref, sin_ref,
-                  weighted_ref, back_proj_ref, mixed_t_ref, w_ref, p_ref, mixed_ref, d_mixed_ref,
+                  weighted_out, back_proj_ref, mixed_t_ref, w_ref, p_ref, mixed_ref, d_mixed_ref,
                   probs, rot, d_rot, slope, back_ref, terms, near_x, near_z, pair_a, pair_b, far_z,
-                  far_x, full, load_sem, send_sem, recv_sem):
+                  far_x, full, load_sem, store_sem, send_sem, recv_sem):
     z, y, x, c = spot()
     side = lax.rem(z, 2)
     x_peer = device(z, y, 1 - x, c)
@@ -1173,11 +1210,15 @@
         incoming(5, i, full.at[b, cols(other_b, part)])
         plans[i][7].start()
 
+    def store(i):
+        b = block(i)
+        return pltpu.make_async_copy(full.at[b], weighted_out.at[b], store_sem.at[i])
+
     def finish(i):
         b = block(i)
         incoming(6, i, full.at[b, give_a])
         incoming(7, i, full.at[b, give_b])
-        weighted_ref[b, :] = full[b, :]
+        store(i).start()
         back_ref[b, :] = lax.dot_general(
             full[b, :], w_ref[...], (((1,), (1,)), ((), ())), preferred_element_type=jnp.float32
         ).astype(jnp.bfloat16)
@@ -1196,6 +1237,8 @@
     for i in range(chunks):
         finish(i)
     attend_back(heads, back_ref, probs, rot, cos_ref, sin_ref, back_proj_ref, slope)
+    for i in range(chunks):
+        store(i).wait()
     for plan in plans:
         for one in plan:
             one.wait_send()
@@ -1220,7 +1263,7 @@
             jax.ShapeDtypeStruct((inner, length), half),
         ),
         in_specs=[vmem] * 2 + [anywhere] * 2 + [vmem] * 3,
-        out_specs=(vmem,) * 3,
+        out_specs=(anywhere, vmem, vmem),
         scratch_shapes=[
             pltpu.VMEM((inner, width), half),
             pltpu.VMEM((inner, width), half),
@@ -1233,6 +1276,7 @@
             narrow,
             whole, quarter, quarter, quarter, quarter, part, part, whole,
             pltpu.SemaphoreType.DMA((2,)),
+            pltpu.SemaphoreType.DMA((chunks,)),
             pltpu.SemaphoreType.DMA((8, chunks)),
             pltpu.SemaphoreType.DMA((8, chunks)),
         ],
@@ -1242,8 +1286,8 @@
     )(projected, d_projected, w_out, p_out, curvature, cosine, sine)
 
 
-def reduce_grid_kernel(n, slots, scale, grid_qkv, grid_out, pick_ref, normed_t_ref, d_proj_ref,
-                       mixed_t_ref, weighted_ref, out_ref, grads, peer, begin, across, onward,
+def reduce_grid_kernel(n, slots, scale, grid_qkv, grid_out, pick_ref, normed_t_in, d_proj_ref,
+                       mixed_t_ref, weighted_ref, out_ref, normed_t_ref, load_sem, grads, peer, begin, across, onward,
                        landed, core_send, core_recv, y_send, y_recv, z_send, z_recv):
     planes = n // 2
     z, y, x, c = spot()
@@ -1254,6 +1298,8 @@
     y_peer = device(z, 1 - y, x, c)
     core_peer = device(z, y, x, 1 - c)
     row = [device(lax.rem(z + i, planes), y, x, c) for i in range(1, planes)]
+    load = pltpu.make_async_copy(normed_t_in, normed_t_ref, load_sem.at[0])
+    load.start()
     greet(row + [core_peer, y_peer])
     cuts = cut_count(slots)
     size = slots // cuts
@@ -1314,6 +1360,7 @@
     peer[total] = jnp.zeros((edge, edge), peer.dtype)
     lax.fori_loop(0, out_cols // group, out_columns, 0)
     hand_over(legs)
+    load.wait()
     for i in range(legs):
         steps = leg_rows // group
         lax.fori_loop(i * steps, (i + 1) * steps, qkv_rows, 0)
@@ -1373,64 +1420,60 @@
     def _():
         for i in (legs,) + tuple(range(legs)):
             core_copy(i).wait_recv()
-        for i in range(planes):
+        def start(i, j):
             base = owner(i, 1 - y) * slots
 
-            def start(j, carry, i=i, base=base):
-                def fill(t):
-                    begin[i * slots + t] = both(pick_ref[base + t]).astype(jnp.bfloat16)
-
-                each(j, fill)
-                y_copy(i, j).start()
+            def fill(t):
+                begin[i * slots + t] = both(pick_ref[base + t]).astype(jnp.bfloat16)
+
+            each(j, fill)
+            y_copy(i, j).start()
+
+        def go(i, j):
+            base = owner(i, y) * slots
+
+            def value(t):
+                return both(pick_ref[base + t]) + across[i * slots + t].astype(jnp.float32)
+
+            def pass_on(t):
+                onward[i, t] = value(t).astype(jnp.bfloat16)
+
+            def join_on(t):
+                onward[i, t] = (value(t) + landed[0, t].astype(jnp.float32)).astype(jnp.bfloat16)
+
+            def last(t):
+                out_ref[t] = (value(t) + landed[late, t].astype(jnp.float32)) * scale
+
+            y_copy(i, j).wait_recv()
+            if i < 2:
+                each(j, pass_on)
+                z_copy(i, j).start()
+            elif i == 2:
+
+                @pl.when(late == 0)
+                def _():
+                    each(j, pass_on)
+
+                @pl.when(late == 1)
+                def _():
+                    z_wait(0, j)
+                    each(j, join_on)
+
+                z_copy(i, j).start()
+            else:
+                z_wait(late, j)
+                each(j, last)
+
+        for i in range(planes + 1):
+
+            def turn_round(j, carry, i=i):
+                if i < planes:
+                    start(i, j)
+                if i > 0:
+                    go(i - 1, j)
                 return carry
 
-            lax.fori_loop(0, cuts, start, 0)
-        for i in range(planes):
-            base = owner(i, y) * slots
-
-            def value(t, i=i, base=base):
-                return both(pick_ref[base + t]) + across[i * slots + t].astype(jnp.float32)
-
-            def go(j, carry, i=i, value=value):
-                y_copy(i, j).wait_recv()
-                if i < 2:
-
-                    def pass_on(t):
-                        onward[i, t] = value(t).astype(jnp.bfloat16)
-
-                    each(j, pass_on)
-                    z_copy(i, j).start()
-                elif i == 2:
-
-                    @pl.when(late == 0)
-                    def _():
-                        def pass_on(t):
-                            onward[i, t] = value(t).astype(jnp.bfloat16)
-
-                        each(j, pass_on)
-
-                    @pl.when(late == 1)
-                    def _():
-                        z_wait(0, j)
-
-                        def pass_on(t):
-                            onward[i, t] = (
-                                value(t) + landed[0, t].astype(jnp.float32)
-                            ).astype(jnp.bfloat16)
-
-                        each(j, pass_on)
-
-                    z_copy(i, j).start()
-                else:
-                    z_wait(late, j)
-
-                    def last(t):
-                        out_ref[t] = (value(t) + landed[late, t].astype(jnp.float32)) * scale
-
-                    each(j, last)
-                return carry
-
-            lax.fori_loop(0, cuts, go, 0)
+            lax.fori_loop(0, cuts, turn_round, 0)
 
         def close(j, carry):
             for i in range(planes):
@@ -1487,9 +1530,12 @@
     return pl.pallas_call(
         functools.partial(reduce_grid_kernel, n, slots, scale, grid_qkv, grid_out),
         out_shape=jax.ShapeDtypeStruct((slots, edge, edge), jnp.float32),
-        in_specs=[pl.BlockSpec(memory_space=pltpu.SMEM)] + [vmem] * 4,
+        in_specs=[pl.BlockSpec(memory_space=pltpu.SMEM), pl.BlockSpec(memory_space=pl.ANY)]
+        + [vmem] * 3,
         out_specs=vmem,
         scratch_shapes=[
+            pltpu.VMEM(normed_t.shape, normed_t.dtype),
+            dma((1,)),
             pltpu.VMEM((total_blocks + 1, edge, edge), jnp.bfloat16),
             pltpu.VMEM((total_blocks + 1, edge, edge), jnp.bfloat16),
             pltpu.VMEM((n // 2 * slots, edge, edge), jnp.bfloat16),

time: 387 us -> 370 us (0.956)
  Pallas kernels: 379 us -> 362 us
    pallas_call x1, Pallas kernels: 181 us -> 170 us  [gather_grid(): pl.pallas_call(functools.partial(gather_grid_kernel, n, slots, grid_qkv,...]
where the time goes in v3:
time: 370 us
  Pallas kernels  362 us (98%)
  local copies, waits for them, and re-layouts  4.01 us (1%)
    pallas_call x1, Pallas kernels, gather_grid(): pl.pallas_call(functools.partial(gather_grid_kernel, n, slots, grid_qkv,...  170 us
    pallas_call x1, Pallas kernels, reduce_grid(): pl.pallas_call(functools.partial(reduce_grid_kernel, n, slots, scale, gri...  104 us
    pallas_call x1, Pallas kernels, square_exchange(): pl.pallas_call(functools.partial(square_kernel, heads), out_shape=(jax.Sh...  87.8 us
  transfers between devices with their start and end apart: 1, of which 0 were waited for; matrix products, arithmetic and copies ran while one was open for 1% of the time, Pallas kernels for 0%

profile of v3, /device:TPU:1, one launch (start us, length us, event | category | flops | bytes accessed | tf_op | source)
XLA Modules:
  0.0 369.8 jit_solution(8714858557080565133)
XLA Ops:
  0.0 0.0 collective-permute-start
  0.0 1.0 fusion.2
  1.0 1.0 pad_maximum_fusion
  2.1 0.0 collective-permute-done
  2.1 0.2 reduce-window.4
  2.3 0.1 convert_reduce_fusion
  2.3 0.1 select_reduce_fusion.2
  2.4 0.6 add_subtract_fusion.slot_ref
  3.0 0.1 select_reduce_fusion.1
  3.1 0.6 add_select_fusion.2.pick_ref
  3.7 170.2 %shard_map.64 = (f32[512,768]{1,0:T(8,128)}, f32[512,768]{1,0:T(8,128)}, bf16[512,4096]{1,0:T(8,128)(2,1)}, bf16[512,4096]{1,0:T(8,128)(2,1)}, bf16[4096,512]{1,0:T(8,128)(2,1)}, /*index=5*/bf16[2,512,512]{2,1,0:T(8,128)(2,1)}) custom-call(s32[320]{0:T(512)} %add_subtract_fusion.slot_ref, bf16[50,128,128]{2,1,0:T(8,128)(2,1)} %bitcast.18, ...), custom_call_target="tpu_custom_call" | custom-call | tf_op jit(solution)/shard_map/pallas_call | solution.py:955
  173.9 87.8 %shard_map.65 = (bf16[512,4096]{1,0:T(8,128)(2,1)}, bf16[512,768]{1,0:T(8,128)(2,1)}, bf16[512,512]{1,0:T(8,128)(2,1)}) custom-call(f32[512,768]{1,0:T(8,128)} %get-tuple-element.15.proj_ref, f32[512,768]{1,0:T(8,128)} %get-tuple-element.16.d_proj_ref, bf16[512,4096]{1,0:T(8,128)(2,1)} %get-tuple-element.17.w_out, ...), custom_call_target="tpu_custom_call" | custom-call | tf_op jit(solution)/shard_map/pallas_call | solution.py:1258
  261.6 104.2 %shard_map.66 = f32[50,128,128]{2,1,0:T(8,128)} custom-call(s32[400]{0:T(512)} %add_select_fusion.2.pick_ref, bf16[4096,512]{1,0:T(8,128)(2,1)} %get-tuple-element.14.normed_t_in, bf16[512,768]{1,0:T(8,128)(2,1)} %get-tuple-element.20.d_proj_ref, bf16[512,512]{1,0:T(8,128)(2,1)} %get-tuple-element.21.mixed_t_ref, ...), custom_call_target="tpu_custom_call" | custom-call | tf_op jit(solution)/shard_map/pallas_call | solution.py:1530
  365.8 4.0 %copy.8 = f32[1,50,128,128]{3,2,1,0:T(8,128)} copy(f32[1,50,128,128]{3,2,1,0:T(8,128)} %bitcast.15) | data formatting | bytes 6553600
  (4 shorter events, 0.0 us)
Async XLA Ops:
  0.0 2.1 collective-permute-start

commit v4 on v3

--- a/solution.py
+++ b/solution.py
@@ -2,6 +2,7 @@
 
 import jax
 import jax.numpy as jnp
+import numpy as np
 from jax import lax
 from jax.experimental import pallas as pl
 from jax.experimental.pallas import tpu as pltpu
@@ -613,7 +614,7 @@
 def gather_grid_kernel(n, slots, grid_qkv, grid_out, slot_ref, w_ref, p_ref, tokens_ref, gain_ref,
                        curv_ref, proj_out, d_proj_ref, wo_out, po_out, normed_t_out, curv_out,
                        held_w, held_p, matrix, normed, wo_ref, po_ref, normed_t_ref, proj_ref,
-                       curv_part, in_sem, out_sem, send_y, send_core, send_z, recv, tok_send,
+                       curv_part, turned, swap_send, swap_recv, in_sem, out_sem, send_y, send_core, send_z, recv, tok_send,
                        tok_recv, relay_send, relay_recv, curv_send, curv_recv):
     planes = n // 2
     z, y, x, c = spot()
@@ -807,15 +808,30 @@
 
         lax.fori_loop(0, normed.shape[0] // rows, some, 0)
 
+    length = normed.shape[0]
+    mid = width // 2
+
     def transpose():
         edge = held_w.shape[-1]
 
         def some(i, carry):
             here = pl.ds(pl.multiple_of(i * edge, edge), edge)
-            normed_t_ref[here, :] = normed[:, here].T
+            mine = pl.ds(pl.multiple_of(c * mid + i * edge, edge), edge)
+            other = pl.ds(pl.multiple_of((1 - c) * mid + i * edge, edge), edge)
+            normed_t_ref[here, :length] = normed[:, mine].T
+            turned[here, :] = normed[:, other].T
             return carry
 
-        lax.fori_loop(0, normed.shape[1] // edge, some, 0)
+        lax.fori_loop(0, mid // edge, some, 0)
+
+    swap = pltpu.make_async_remote_copy(
+        src_ref=turned,
+        dst_ref=normed_t_ref.at[:, pl.ds(length, length)],
+        send_sem=swap_send.at[0],
+        recv_sem=swap_recv.at[0],
+        device_id=core_peer,
+        device_id_type=pl.DeviceIdType.MESH,
+    )
 
     def project(result_ref):
         rows = 256
@@ -880,7 +896,7 @@
         step(0, j)
         if j == 0:
             transpose()
-            stores[0].start()
+            swap.start()
     keep_own(0)
     def first_proj():
         project(proj_ref)
@@ -912,6 +928,8 @@
             curv_copy(i).wait_recv()
 
     stores[4].start()
+    swap.wait_recv()
+    stores[0].start()
     unpack_qkv(1)
     project(d_proj_ref)
 
@@ -937,6 +955,7 @@
             for copy in spoke_own(*one):
                 copy.wait_send()
 
+    swap.wait_send()
     for store in stores:
         store.wait()
 
@@ -946,7 +965,7 @@
     cuts = cut_count(slots)
     length, width = tokens.shape
     proj = jax.ShapeDtypeStruct((length, grid_qkv[1] * edge), jnp.float32)
-    turned = jax.ShapeDtypeStruct((width, length), jnp.bfloat16)
+    turned = jax.ShapeDtypeStruct((width // 2, 2 * length), jnp.bfloat16)
     out = jax.ShapeDtypeStruct((grid_out[0] * edge, grid_out[1] * edge), jnp.bfloat16)
     shard = (2, length, width // 8)
     vmem = pl.BlockSpec(memory_space=pltpu.VMEM)
@@ -967,6 +986,9 @@
             pltpu.VMEM(turned.shape, turned.dtype),
             pltpu.VMEM(proj.shape, proj.dtype),
             pltpu.VMEM(shard, jnp.bfloat16),
+            pltpu.VMEM((width // 2, length), jnp.bfloat16),
+            dma((1,)),
+            dma((1,)),
             dma((3,)),
             dma((5,)),
             dma((n // 2, 2 * cuts)),
@@ -987,9 +1009,14 @@
 
 
 def turn_tables(length, head_dim):
-    cosine, sine = rotary(length, head_dim)
-    cosine, sine = cosine[:, 0, :], sine[:, 0, :]
-    return jnp.concatenate([cosine, cosine], axis=1), jnp.concatenate([-sine, sine], axis=1)
+    half_dim = head_dim // 2
+    frequency = np.exp(-np.log(THETA) * 2.0 * np.arange(half_dim) / head_dim).astype(np.float32)
+    angles = np.arange(length, dtype=np.float32)[:, None] * frequency[None, :]
+    cosine, sine = np.cos(angles), np.sin(angles)
+    return (
+        jnp.asarray(np.concatenate([cosine, cosine], axis=1), jnp.float32),
+        jnp.asarray(np.concatenate([-sine, sine], axis=1), jnp.float32),
+    )
 
 
 def turn(values, cosine, sine):
@@ -1105,9 +1132,10 @@
 
 
 def square_kernel(heads, proj_ref, d_proj_ref, w_out, p_out, curv_ref, cos_ref, sin_ref,
-                  weighted_out, back_proj_ref, mixed_t_ref, w_ref, p_ref, mixed_ref, d_mixed_ref,
+                  weighted_out, back_proj_ref, mixed_t_out, mixed_t, theirs, w_ref, p_ref, mixed_ref, d_mixed_ref,
                   probs, rot, d_rot, slope, back_ref, terms, near_x, near_z, pair_a, pair_b, far_z,
-                  far_x, full, load_sem, store_sem, send_sem, recv_sem):
+                  far_x, full, load_sem, store_sem, swap_send, swap_recv, send_sem,
+                  recv_sem):
     z, y, x, c = spot()
     side = lax.rem(z, 2)
     x_peer = device(z, y, 1 - x, c)
@@ -1118,16 +1146,32 @@
     ]
     for load in loads:
         load.start()
-    greet([x_peer, z_peer])
+    core_peer = device(z, y, x, 1 - c)
+    greet([x_peer, z_peer, core_peer])
     attend(
-        heads, proj_ref, d_proj_ref, cos_ref, sin_ref, mixed_ref, d_mixed_ref, mixed_t_ref, probs,
-        rot, d_rot,
+        heads, proj_ref, d_proj_ref, cos_ref, sin_ref, mixed_ref, d_mixed_ref, mixed_t, probs, rot,
+        d_rot,
     )
+    length, width = terms.shape
+    chunks = recv_sem.shape[1]
+
+    def swap(i, here, there):
+        return pltpu.make_async_remote_copy(
+            src_ref=here,
+            dst_ref=there,
+            send_sem=swap_send.at[i],
+            recv_sem=swap_recv.at[i],
+            device_id=core_peer,
+            device_id_type=pl.DeviceIdType.MESH,
+        )
+
+    swap_mixed = swap(
+        chunks, mixed_t.at[:, pl.ds(0, length)], mixed_t.at[:, pl.ds(length, length)]
+    )
+    swap_mixed.start()
     for load in loads:
         load.wait()
-    length, width = terms.shape
     quarter, part = width // 4, width // 8
-    chunks = recv_sem.shape[1]
     rows = length // chunks
 
     def block(i):
@@ -1210,15 +1254,28 @@
         incoming(5, i, full.at[b, cols(other_b, part)])
         plans[i][7].start()
 
+    mid = width // 2
+
     def store(i):
         b = block(i)
-        return pltpu.make_async_copy(full.at[b], weighted_out.at[b], store_sem.at[i])
+        return pltpu.make_async_copy(
+            full.at[b, cols(c * mid, mid)], weighted_out.at[b], store_sem.at[i]
+        )
+
+    def store_theirs(i):
+        there = weighted_out.at[pl.ds(length + i * rows, rows)]
+        return pltpu.make_async_copy(theirs.at[block(i)], there, store_sem.at[chunks + i])
+
+    def swap_weighted(i):
+        b = block(i)
+        return swap(i, full.at[b, cols((1 - c) * mid, mid)], theirs.at[b])
 
     def finish(i):
         b = block(i)
         incoming(6, i, full.at[b, give_a])
         incoming(7, i, full.at[b, give_b])
         store(i).start()
+        swap_weighted(i).start()
         back_ref[b, :] = lax.dot_general(
             full[b, :], w_ref[...], (((1,), (1,)), ((), ())), preferred_element_type=jnp.float32
         ).astype(jnp.bfloat16)
@@ -1236,9 +1293,19 @@
             widen(i - 3)
     for i in range(chunks):
         finish(i)
+    swap_mixed.wait_recv()
+    store_mixed = pltpu.make_async_copy(mixed_t, mixed_t_out, store_sem.at[2 * chunks])
+    store_mixed.start()
+    for i in range(chunks):
+        swap_weighted(i).wait_recv()
+        store_theirs(i).start()
     attend_back(heads, back_ref, probs, rot, cos_ref, sin_ref, back_proj_ref, slope)
+    store_mixed.wait()
     for i in range(chunks):
         store(i).wait()
+        store_theirs(i).wait()
+        swap_weighted(i).wait_send()
+    swap_mixed.wait_send()
     for plan in plans:
         for one in plan:
             one.wait_send()
@@ -1258,13 +1325,15 @@
     return pl.pallas_call(
         functools.partial(square_kernel, heads),
         out_shape=(
-            jax.ShapeDtypeStruct((length, width), half),
+            jax.ShapeDtypeStruct((2 * length, width // 2), half),
             jax.ShapeDtypeStruct((length, inputs), half),
-            jax.ShapeDtypeStruct((inner, length), half),
+            jax.ShapeDtypeStruct((inner, 2 * length), half),
         ),
         in_specs=[vmem] * 2 + [anywhere] * 2 + [vmem] * 3,
-        out_specs=(anywhere, vmem, vmem),
+        out_specs=(anywhere, vmem, anywhere),
         scratch_shapes=[
+            pltpu.VMEM((inner, 2 * length), half),
+            pltpu.VMEM((length, width // 2), half),
             pltpu.VMEM((inner, width), half),
             pltpu.VMEM((inner, width), half),
             narrow,
@@ -1276,7 +1345,9 @@
             narrow,
             whole, quarter, quarter, quarter, quarter, part, part, whole,
             pltpu.SemaphoreType.DMA((2,)),
-            pltpu.SemaphoreType.DMA((chunks,)),
+            pltpu.SemaphoreType.DMA((2 * chunks + 1,)),
+            pltpu.SemaphoreType.DMA((chunks + 1,)),
+            pltpu.SemaphoreType.DMA((chunks + 1,)),
             pltpu.SemaphoreType.DMA((8, chunks)),
             pltpu.SemaphoreType.DMA((8, chunks)),
         ],
@@ -1286,8 +1357,9 @@
     )(projected, d_projected, w_out, p_out, curvature, cosine, sine)
 
 
-def reduce_grid_kernel(n, slots, scale, grid_qkv, grid_out, pick_ref, normed_t_in, d_proj_ref,
-                       mixed_t_ref, weighted_ref, out_ref, normed_t_ref, load_sem, grads, peer, begin, across, onward,
+def reduce_grid_kernel(n, slots, scale, grid_qkv, grid_out, pick_ref, normed_t_in, d_proj_in,
+                       mixed_t_ref, weighted_ref, out_ref, d_proj_ref, swap_sem,
+                       normed_t_ref, load_sem, grads, begin, across, onward,
                        landed, core_send, core_recv, y_send, y_recv, z_send, z_recv):
     planes = n // 2
     z, y, x, c = spot()
@@ -1300,25 +1372,39 @@
     row = [device(lax.rem(z + i, planes), y, x, c) for i in range(1, planes)]
     load = pltpu.make_async_copy(normed_t_in, normed_t_ref, load_sem.at[0])
     load.start()
+    own_rows = d_proj_in.shape[0]
+    d_proj_ref[:own_rows] = d_proj_in[...]
     greet(row + [core_peer, y_peer])
+    swap = pltpu.make_async_remote_copy(
+        src_ref=d_proj_in,
+        dst_ref=d_proj_ref.at[pl.ds(own_rows, own_rows)],
+        send_sem=swap_sem.at[0],
+        recv_sem=swap_sem.at[1],
+        device_id=core_peer,
+        device_id_type=pl.DeviceIdType.MESH,
+    )
+    swap.start()
     cuts = cut_count(slots)
     size = slots // cuts
     rows, cols = grid_qkv
     out_rows, out_cols = grid_out
     total = rows * cols + out_rows * out_cols
     edge = out_ref.shape[-1]
-    legs = core_send.shape[0] - 1
-    leg_rows = rows // legs
+    legs = core_send.shape[0] - out_rows
+    leg_rows = rows // 2 // legs
     group = 2
+    giver = 1 - lax.rem(z, 2)
 
     def core_copy(i):
-        if i == legs:
-            here = pl.ds(rows * cols, out_rows * out_cols)
+        if i < out_rows:
+            count = out_cols // 2
+            here = pl.ds(rows * cols + i * out_cols + giver * count, count)
         else:
-            here = pl.ds(i * leg_rows * cols, leg_rows * cols)
+            count = leg_rows * cols
+            here = pl.ds((giver * legs + i - out_rows) * count, count)
         return pltpu.make_async_remote_copy(
             src_ref=grads.at[here],
-            dst_ref=peer.at[here],
+            dst_ref=grads.at[here],
             send_sem=core_send.at[i],
             recv_sem=core_recv.at[i],
             device_id=core_peer,
@@ -1333,9 +1419,8 @@
         ).astype(jnp.bfloat16)
         for r in range(out_rows):
             for k in range(group):
-                grads[rows * cols + r * out_cols + i * group + k] = block[
-                    r * edge:(r + 1) * edge, k * edge:(k + 1) * edge
-                ]
+                at = rows * cols + r * out_cols + c * (out_cols // 2) + i * group + k
+                grads[at] = block[r * edge:(r + 1) * edge, k * edge:(k + 1) * edge]
         return carry
 
     def qkv_rows(i, carry):
@@ -1346,7 +1431,7 @@
         ).astype(jnp.bfloat16)
         for r in range(group):
             for k in range(cols):
-                grads[(i * group + r) * cols + k] = block[
+                grads[(c * (rows // 2) + i * group + r) * cols + k] = block[
                     r * edge:(r + 1) * edge, k * edge:(k + 1) * edge
                 ]
         return carry
@@ -1357,14 +1442,15 @@
             core_copy(i).start()
 
     grads[total] = jnp.zeros((edge, edge), grads.dtype)
-    peer[total] = jnp.zeros((edge, edge), peer.dtype)
-    lax.fori_loop(0, out_cols // group, out_columns, 0)
-    hand_over(legs)
+    lax.fori_loop(0, out_cols // 2 // group, out_columns, 0)
+    for i in range(out_rows):
+        hand_over(i)
     load.wait()
+    swap.wait()
     for i in range(legs):
         steps = leg_rows // group
         lax.fori_loop(i * steps, (i + 1) * steps, qkv_rows, 0)
-        hand_over(i)
+        hand_over(out_rows + i)
 
     def owner(i, at_y):
         first = (3, 2, 1, 0)[i]
@@ -1372,8 +1458,8 @@
         o = (1 - late) * first + late * second
         return 2 * mirrored(o, c, planes) + at_y
 
-    def both(index):
-        return grads[index].astype(jnp.float32) + peer[index].astype(jnp.float32)
+    def block_sum(index):
+        return grads[index].astype(jnp.float32)
 
     def y_copy(i, j):
         here = pl.ds(i * slots + j * size, size)
@@ -1418,13 +1504,13 @@
 
     @pl.when(hub)
     def _():
-        for i in (legs,) + tuple(range(legs)):
+        for i in range(out_rows + legs):
             core_copy(i).wait_recv()
         def start(i, j):
             base = owner(i, 1 - y) * slots
 
             def fill(t):
-                begin[i * slots + t] = both(pick_ref[base + t]).astype(jnp.bfloat16)
+                begin[i * slots + t] = grads[pick_ref[base + t]]
 
             each(j, fill)
             y_copy(i, j).start()
@@ -1433,7 +1519,7 @@
             base = owner(i, y) * slots
 
             def value(t):
-                return both(pick_ref[base + t]) + across[i * slots + t].astype(jnp.float32)
+                return block_sum(pick_ref[base + t]) + across[i * slots + t].astype(jnp.float32)
 
             def pass_on(t):
                 onward[i, t] = value(t).astype(jnp.bfloat16)
@@ -1515,7 +1601,7 @@
 
             lax.fori_loop(0, cuts, go, 0)
 
-        for i in range(legs + 1):
+        for i in range(out_rows + legs):
             core_copy(i).wait_send()
 
 
@@ -1534,16 +1620,17 @@
         + [vmem] * 3,
         out_specs=vmem,
         scratch_shapes=[
+            pltpu.VMEM((2 * d_proj.shape[0], d_proj.shape[1]), d_proj.dtype),
+            dma((2,)),
             pltpu.VMEM(normed_t.shape, normed_t.dtype),
             dma((1,)),
-            pltpu.VMEM((total_blocks + 1, edge, edge), jnp.bfloat16),
             pltpu.VMEM((total_blocks + 1, edge, edge), jnp.bfloat16),
             pltpu.VMEM((n // 2 * slots, edge, edge), jnp.bfloat16),
             pltpu.VMEM((n // 2 * slots, edge, edge), jnp.bfloat16),
             pltpu.VMEM((3, slots, edge, edge), jnp.bfloat16),
             pltpu.VMEM((2, slots, edge, edge), jnp.bfloat16),
-            dma((legs + 1,)),
-            dma((legs + 1,)),
+            dma((grid_out[0] + legs,)),
+            dma((grid_out[0] + legs,)),
             dma((n // 2, cuts)),
             dma((n // 2, cuts)),
             dma((3, cuts)),

time: 370 us -> 362 us (0.978)
  Pallas kernels: 362 us -> 354 us
    pallas_call x1, Pallas kernels: 104 us -> 95.8 us  [reduce_grid(): pl.pallas_call(functools.partial(reduce_grid_kernel, n, slots, scale, gri...]
  transfers between devices with their start and end apart: 1 -> 1, of which waited for: 0 -> 1; matrix products, arithmetic and copies ran while one was open for 1% -> 0% of each run, Pallas kernels for 0% -> 0%
where the time goes in v4:
time: 362 us; the launch traced here: 361 us
  Pallas kernels  354 us (98%)
  local copies, waits for them, and re-layouts  4.01 us (1%)
    pallas_call x1, Pallas kernels, gather_grid(): pl.pallas_call(functools.partial(gather_grid_kernel, n, slots, grid_qkv,...  170 us
    pallas_call x1, Pallas kernels, reduce_grid(): pl.pallas_call(functools.partial(reduce_grid_kernel, n, slots, scale, gri...  95.8 us
    pallas_call x1, Pallas kernels, square_exchange(): pl.pallas_call(functools.partial(square_kernel, heads), out_shape=(jax.Sh...  88.4 us
  transfers between devices with their start and end apart: 1, of which 1 were waited for; matrix products, arithmetic and copies ran while one was open for 0% of the time, Pallas kernels for 0%

profile of v4, /device:TPU:1, one launch (start us, length us, event | category | flops | bytes accessed | tf_op | source)
XLA Modules:
  0.0 361.3 jit_solution(10321678646920706261)
XLA Ops:
  0.0 0.0 collective-permute-start
  0.0 1.3 collective-permute-done
  1.3 0.2 reduce-window.4
  1.5 0.1 convert_reduce_fusion
  1.6 0.1 select_reduce_fusion.2
  1.7 0.6 add_subtract_fusion.slot_ref
  2.3 0.1 select_reduce_fusion.1
  2.3 0.6 add_select_fusion.2.pick_ref
  2.9 170.2 %shard_map.82 = (f32[512,768]{1,0:T(8,128)}, f32[512,768]{1,0:T(8,128)}, bf16[512,4096]{1,0:T(8,128)(2,1)}, bf16[512,4096]{1,0:T(8,128)(2,1)}, bf16[2048,1024]{1,0:T(8,128)(2,1)}, /*index=5*/bf16[2,512,512]{2,1,0:T(8,128)(2,1)}) custom-call(s32[320]{0:T(512)} %add_subtract_fusion.slot_ref, bf16[50,128,128]{2,1,0:T(8,128)(2,1)} %bitcast.18, ...), custom_call_target="tpu_custom_call" | custom-call | tf_op jit(solution)/shard_map/pallas_call | solution.py:974
  173.1 88.4 %shard_map.83 = (bf16[1024,2048]{1,0:T(8,128)(2,1)}, bf16[512,768]{1,0:T(8,128)(2,1)}, bf16[512,1024]{1,0:T(8,128)(2,1)}) custom-call(f32[512,768]{1,0:T(8,128)} %get-tuple-element.15.proj_ref, f32[512,768]{1,0:T(8,128)} %get-tuple-element.16.d_proj_ref, bf16[512,4096]{1,0:T(8,128)(2,1)} %get-tuple-element.17.w_out, ...), custom_call_target="tpu_custom_call" | custom-call | tf_op jit(solution)/shard_map/pallas_call | solution.py:1325
  261.5 95.8 %shard_map.84 = f32[50,128,128]{2,1,0:T(8,128)} custom-call(s32[400]{0:T(512)} %add_select_fusion.2.pick_ref, bf16[2048,1024]{1,0:T(8,128)(2,1)} %get-tuple-element.14.normed_t_in, bf16[512,768]{1,0:T(8,128)(2,1)} %get-tuple-element.20.d_proj_in, bf16[512,1024]{1,0:T(8,128)(2,1)} %get-tuple-element.21.mixed_t_ref, ...), custom_call_target="tpu_custom_call" | custom-call | tf_op jit(solution)/shard_map/pallas_call | solution.py:1616
  357.3 4.0 %copy.10 = f32[1,50,128,128]{3,2,1,0:T(8,128)} copy(f32[1,50,128,128]{3,2,1,0:T(8,128)} %bitcast.15) | data formatting | bytes 6553600
  (3 shorter events, 0.0 us)
Async XLA Ops:
  0.0 1.3 collective-permute-start

commit v5 on v4

--- a/solution.py
+++ b/solution.py
@@ -1023,63 +1023,59 @@
     return values * cosine + pltpu.roll(values, values.shape[1] // 2, 1) * sine
 
 
-def attend(heads, proj_ref, d_proj_ref, cos_ref, sin_ref, mixed_ref, d_mixed_ref, mixed_t_ref,
-           probs_ref, rot_ref, d_rot):
-    length = proj_ref.shape[0]
-    hd = cos_ref.shape[1]
+def spin(heads, hd, source, target, cos_ref, sin_ref):
+    val_at = (heads + 1) * hd
+
+    def some(h, carry):
+        here = pl.ds(pl.multiple_of(h * hd, hd), hd)
+        target[:, here] = turn(source[:, here], cos_ref[...], sin_ref[...]).astype(jnp.bfloat16)
+        return carry
+
+    lax.fori_loop(0, heads + 1, some, 0)
+    target[:, val_at:] = source[:, val_at:].astype(jnp.bfloat16)
+
+
+def attend(heads, hd, first, tile, mixed_ref, d_mixed_ref, mixed_t_ref, probs_ref, rot_ref, d_rot):
+    length = rot_ref.shape[0]
     key_at = heads * hd
     val_at = key_at + hd
     scale = hd ** -0.5
-
-    def spin(source, target):
-        def some(h, carry):
-            here = pl.ds(pl.multiple_of(h * hd, hd), hd)
-            target[:, here] = turn(source[:, here], cos_ref[...], sin_ref[...]).astype(jnp.bfloat16)
-            return carry
-
-        lax.fori_loop(0, heads + 1, some, 0)
-        target[:, val_at:] = source[:, val_at:].astype(jnp.bfloat16)
-
-    spin(proj_ref, rot_ref)
-    spin(d_proj_ref, d_rot)
-    tile = hd
+    rows = slice(first, first + tile)
+    span = first + tile
 
     def head(h, carry):
         here = pl.ds(pl.multiple_of(h * hd, hd), hd)
-        for i in range(length // tile):
-            rows = slice(i * tile, (i + 1) * tile)
-            span = (i + 1) * tile
-            q, dq = rot_ref[rows, here], d_rot[rows, here]
-            k, dk = rot_ref[:span, key_at:val_at], d_rot[:span, key_at:val_at]
-            v, dv = rot_ref[:span, val_at:], d_rot[:span, val_at:]
-            contract = (((1,), (1,)), ((), ()))
-            scores = lax.dot_general(q, k, contract, preferred_element_type=jnp.float32) * scale
-            slopes = lax.dot_general(
-                jnp.concatenate([dq, q], axis=1),
-                jnp.concatenate([k, dk], axis=1),
-                contract,
-                preferred_element_type=jnp.float32,
-            ) * scale
-            at_row = i * tile + lax.broadcasted_iota(jnp.int32, (tile, span), 0)
-            at_col = lax.broadcasted_iota(jnp.int32, (tile, span), 1)
-            seen = at_row >= at_col
-            scores = jnp.where(seen, scores, NEGATIVE)
-            slopes = jnp.where(seen, slopes, 0.0)
-            raised = jnp.exp(scores - jnp.max(scores, axis=1, keepdims=True))
-            probs = raised / jnp.sum(raised, axis=1, keepdims=True)
-            d_probs = probs * (slopes - jnp.sum(probs * slopes, axis=1, keepdims=True))
-            probs = probs.astype(jnp.bfloat16)
-            d_probs = d_probs.astype(jnp.bfloat16)
-            probs_ref[h, rows, :span] = probs
-            if span < length:
-                probs_ref[h, rows, span:] = jnp.zeros((tile, length - span), jnp.bfloat16)
-            mixed = jnp.dot(probs, v, preferred_element_type=jnp.float32).astype(jnp.bfloat16)
-            mixed_ref[rows, here] = mixed
-            mixed_t_ref[here, rows] = mixed.T
-            d_mixed_ref[rows, here] = (
-                jnp.dot(d_probs, v, preferred_element_type=jnp.float32)
-                + jnp.dot(probs, dv, preferred_element_type=jnp.float32)
-            ).astype(jnp.bfloat16)
+        q, dq = rot_ref[rows, here], d_rot[rows, here]
+        k, dk = rot_ref[:span, key_at:val_at], d_rot[:span, key_at:val_at]
+        v, dv = rot_ref[:span, val_at:], d_rot[:span, val_at:]
+        contract = (((1,), (1,)), ((), ()))
+        scores = lax.dot_general(q, k, contract, preferred_element_type=jnp.float32) * scale
+        slopes = lax.dot_general(
+            jnp.concatenate([dq, q], axis=1),
+            jnp.concatenate([k, dk], axis=1),
+            contract,
+            preferred_element_type=jnp.float32,
+        ) * scale
+        at_row = first + lax.broadcasted_iota(jnp.int32, (tile, span), 0)
+        at_col = lax.broadcasted_iota(jnp.int32, (tile, span), 1)
+        seen = at_row >= at_col
+        scores = jnp.where(seen, scores, NEGATIVE)
+        slopes = jnp.where(seen, slopes, 0.0)
+        raised = jnp.exp(scores - jnp.max(scores, axis=1, keepdims=True))
+        probs = raised / jnp.sum(raised, axis=1, keepdims=True)
+        d_probs = probs * (slopes - jnp.sum(probs * slopes, axis=1, keepdims=True))
+        probs = probs.astype(jnp.bfloat16)
+        d_probs = d_probs.astype(jnp.bfloat16)
+        probs_ref[h, rows, :span] = probs
+        if span < length:
+            probs_ref[h, rows, span:] = jnp.zeros((tile, length - span), jnp.bfloat16)
+        mixed = jnp.dot(probs, v, preferred_element_type=jnp.float32).astype(jnp.bfloat16)
+        mixed_ref[rows, here] = mixed
+        mixed_t_ref[here, rows] = mixed.T
+        d_mixed_ref[rows, here] = (
+            jnp.dot(d_probs, v, preferred_element_type=jnp.float32)
+            + jnp.dot(probs, dv, preferred_element_type=jnp.float32)
+        ).astype(jnp.bfloat16)
         return carry
 
     lax.fori_loop(0, heads, head, 0)
@@ -1148,10 +1144,9 @@
         load.start()
     core_peer = device(z, y, x, 1 - c)
     greet([x_peer, z_peer, core_peer])
-    attend(
-        heads, proj_ref, d_proj_ref, cos_ref, sin_ref, mixed_ref, d_mixed_ref, mixed_t, probs, rot,
-        d_rot,
-    )
+    hd = cos_ref.shape[1]
+    spin(heads, hd, proj_ref, rot, cos_ref, sin_ref)
+    spin(heads, hd, d_proj_ref, d_rot, cos_ref, sin_ref)
     length, width = terms.shape
     chunks = recv_sem.shape[1]
 
@@ -1168,11 +1163,11 @@
     swap_mixed = swap(
         chunks, mixed_t.at[:, pl.ds(0, length)], mixed_t.at[:, pl.ds(length, length)]
     )
-    swap_mixed.start()
-    for load in loads:
-        load.wait()
+    rows = length // chunks
+    tile = min(hd, length)
+    tiles = length // tile
+    per = chunks // tiles
     quarter, part = width // 4, width // 8
-    rows = length // chunks
 
     def block(i):
         return pl.ds(i * rows, rows)
@@ -1212,14 +1207,25 @@
     def incoming(kind, i, there):
         copy(kind, i, there, there, x_peer).wait_recv()
 
+    def group(i):
+        return pl.ds(i * tile, tile)
+
     def terms_of(i):
-        tile = width // 4
+        attend(
+            heads, hd, i * tile, tile, mixed_ref, d_mixed_ref, mixed_t, probs, rot, d_rot
+        )
+        if i == 0:
+            for load in loads:
+                load.wait()
+        if i == tiles - 1:
+            swap_mixed.start()
+        b = group(i)
 
         def columns(j, carry):
-            here = pl.ds(pl.multiple_of(j * tile, tile), tile)
-            terms[block(i), here] = (
-                jnp.dot(d_mixed_ref[block(i), :], w_ref[:, here], preferred_element_type=jnp.float32)
-                + jnp.dot(mixed_ref[block(i), :], p_ref[:, here], preferred_element_type=jnp.float32)
+            here = pl.ds(pl.multiple_of(j * quarter, quarter), quarter)
+            terms[b, here] = (
+                jnp.dot(d_mixed_ref[b, :], w_ref[:, here], preferred_element_type=jnp.float32)
+                + jnp.dot(mixed_ref[b, :], p_ref[:, here], preferred_element_type=jnp.float32)
             ).astype(jnp.bfloat16)
             return carry
 
@@ -1276,13 +1282,16 @@
         incoming(7, i, full.at[b, give_b])
         store(i).start()
         swap_weighted(i).start()
-        back_ref[b, :] = lax.dot_general(
-            full[b, :], w_ref[...], (((1,), (1,)), ((), ())), preferred_element_type=jnp.float32
-        ).astype(jnp.bfloat16)
+        if i % per == per - 1:
+            g = group(i // per)
+            back_ref[g, :] = lax.dot_general(
+                full[g, :], w_ref[...], (((1,), (1,)), ((), ())), preferred_element_type=jnp.float32
+            ).astype(jnp.bfloat16)
 
     for i in range(chunks + 3):
         if i < chunks:
-            terms_of(i)
+            if i % per == 0:
+                terms_of(i // per)
             plans[i][0].start()
             plans[i][1].start()
         if 0 <= i - 1 < chunks:
@@ -1357,7 +1366,7 @@
     )(projected, d_projected, w_out, p_out, curvature, cosine, sine)
 
 
-def reduce_grid_kernel(n, slots, scale, grid_qkv, grid_out, pick_ref, normed_t_in, d_proj_in,
+def reduce_grid_kernel(n, slots, grid_qkv, grid_out, pick_ref, normed_t_in, d_proj_in,
                        mixed_t_ref, weighted_ref, out_ref, d_proj_ref, swap_sem,
                        normed_t_ref, load_sem, grads, begin, across, onward,
                        landed, core_send, core_recv, y_send, y_recv, z_send, z_recv):
@@ -1528,7 +1537,7 @@
                 onward[i, t] = (value(t) + landed[0, t].astype(jnp.float32)).astype(jnp.bfloat16)
 
             def last(t):
-                out_ref[t] = (value(t) + landed[late, t].astype(jnp.float32)) * scale
+                out_ref[t] = (value(t) + landed[late, t].astype(jnp.float32)).astype(jnp.bfloat16)
 
             y_copy(i, j).wait_recv()
             if i < 2:
@@ -1581,7 +1590,7 @@
                 def last(t):
                     out_ref[t] = (
                         landed[0, t].astype(jnp.float32) + landed[1, t].astype(jnp.float32)
-                    ) * scale
+                    ).astype(jnp.bfloat16)
 
                 each(j, last)
                 return carry
@@ -1594,7 +1603,7 @@
                 z_wait(0, j)
 
                 def last(t):
-                    out_ref[t] = landed[0, t].astype(jnp.float32) * scale
+                    out_ref[t] = landed[0, t]
 
                 each(j, last)
                 return carry
@@ -1605,7 +1614,7 @@
             core_copy(i).wait_send()
 
 
-def reduce_grid(picked, normed_t, d_proj, mixed_t, weighted, n, scale, grid_qkv, grid_out):
+def reduce_grid(picked, normed_t, d_proj, mixed_t, weighted, n, grid_qkv, grid_out):
     slots = picked.shape[0] // n
     edge = BLK
     total_blocks = grid_qkv[0] * grid_qkv[1] + grid_out[0] * grid_out[1]
@@ -1614,8 +1623,8 @@
     vmem = pl.BlockSpec(memory_space=pltpu.VMEM)
     dma = pltpu.SemaphoreType.DMA
     return pl.pallas_call(
-        functools.partial(reduce_grid_kernel, n, slots, scale, grid_qkv, grid_out),
-        out_shape=jax.ShapeDtypeStruct((slots, edge, edge), jnp.float32),
+        functools.partial(reduce_grid_kernel, n, slots, grid_qkv, grid_out),
+        out_shape=jax.ShapeDtypeStruct((slots, edge, edge), jnp.bfloat16),
         in_specs=[pl.BlockSpec(memory_space=pltpu.SMEM), pl.BlockSpec(memory_space=pl.ANY)]
         + [vmem] * 3,
         out_specs=vmem,
@@ -1687,18 +1696,18 @@
     owner_first = jnp.sum(jnp.where(owner_hot, starts[None, :], 0), axis=1)
     own_count = jnp.sum(jnp.where(owner_hot, counts[None, :], 0), axis=1)
     picked = jnp.where(place < own_count, owner_first + place, total_blocks).astype(jnp.int32)
-    scaled = reduce_grid(
+    summed = reduce_grid(
         picked,
         normed_t,
         back_projected,
         mixed_t,
         weighted,
         n_owners,
-        (length * n_owners) ** -0.5,
         grid_qkv,
         grid_out,
     )
-    return scaled.reshape(1, slots, BLK, BLK)
+    scale = (length * n_owners) ** -0.5
+    return summed.astype(jnp.float32).reshape(1, slots, BLK, BLK) * scale
 
 
 def solution(mesh):

time: 362 us -> 356 us (0.983)
  local copies, waits for them, and re-layouts: 4.01 us -> 0 us
  Pallas kernels: 354 us -> 350 us
    pallas_call x1, Pallas kernels: 88.4 us -> 84.3 us  [square_exchange(): pl.pallas_call(functools.partial(square_kernel, heads), out_shape=(jax.Sh...]
    unnamed x1 -> x0, local copies, waits for them, and re-layouts: 4.01 us -> none
where the time goes in v5:
time: 356 us
  Pallas kernels  350 us (98%)
  other arithmetic  5.19 us (1%)
    pallas_call x1, Pallas kernels, gather_grid(): pl.pallas_call(functools.partial(gather_grid_kernel, n, slots, grid_qkv,...  170 us
    pallas_call x1, Pallas kernels, reduce_grid(): pl.pallas_call(functools.partial(reduce_grid_kernel, n, slots, grid_qkv,...  95.2 us
    pallas_call x1, Pallas kernels, square_exchange(): pl.pallas_call(functools.partial(square_kernel, heads), out_shape=(jax.Sh...  84.3 us
  transfers between devices with their start and end apart: 1, of which 1 were waited for; matrix products, arithmetic and copies ran while one was open for 0% of the time, Pallas kernels for 0%

profile of v5, /device:TPU:1, one launch (start us, length us, event | category | flops | bytes accessed | tf_op | source)
XLA Modules:
  0.0 356.2 jit_solution(17450397957079698357)
XLA Ops:
  0.0 0.0 collective-permute-start
  0.0 1.3 collective-permute-done
  1.3 0.2 reduce-window.4
  1.5 0.1 convert_reduce_fusion
  1.6 0.1 select_reduce_fusion.2
  1.7 0.6 add_subtract_fusion.slot_ref
  2.3 0.1 select_reduce_fusion.1
  2.3 0.6 add_select_fusion.2.pick_ref
  2.9 170.2 %shard_map.82 = (f32[512,768]{1,0:T(8,128)}, f32[512,768]{1,0:T(8,128)}, bf16[512,4096]{1,0:T(8,128)(2,1)}, bf16[512,4096]{1,0:T(8,128)(2,1)}, bf16[2048,1024]{1,0:T(8,128)(2,1)}, /*index=5*/bf16[2,512,512]{2,1,0:T(8,128)(2,1)}) custom-call(s32[320]{0:T(512)} %add_subtract_fusion.slot_ref, bf16[50,128,128]{2,1,0:T(8,128)(2,1)} %bitcast.18, ...), custom_call_target="tpu_custom_call" | custom-call | tf_op jit(solution)/shard_map/pallas_call | solution.py:974
  173.1 84.3 %shard_map.83 = (bf16[1024,2048]{1,0:T(8,128)(2,1)}, bf16[512,768]{1,0:T(8,128)(2,1)}, bf16[512,1024]{1,0:T(8,128)(2,1)}) custom-call(f32[512,768]{1,0:T(8,128)} %get-tuple-element.15.proj_ref, f32[512,768]{1,0:T(8,128)} %get-tuple-element.16.d_proj_ref, bf16[512,4096]{1,0:T(8,128)(2,1)} %get-tuple-element.17.w_out, ...), custom_call_target="tpu_custom_call" | custom-call | tf_op jit(solution)/shard_map/pallas_call | solution.py:1334
  257.5 95.2 %shard_map.84 = bf16[50,128,128]{2,1,0:T(8,128)(2,1)} custom-call(s32[400]{0:T(512)} %add_select_fusion.2.pick_ref, bf16[2048,1024]{1,0:T(8,128)(2,1)} %get-tuple-element.14.normed_t_in, bf16[512,768]{1,0:T(8,128)(2,1)} %get-tuple-element.20.d_proj_in, bf16[512,1024]{1,0:T(8,128)(2,1)} %get-tuple-element.21.mixed_t_ref, ...), custom_call_target="tpu_custom_call" | custom-call | tf_op jit(solution)/shard_map/pallas_call | solution.py:1625
  352.7 3.5 multiply_bitcast_fusion
  (3 shorter events, 0.0 us)
Async XLA Ops:
  0.0 1.3 collective-permute-start

commit v6 on v5

--- a/solution.py
+++ b/solution.py
@@ -607,8 +607,11 @@
     return x * (width // 4) + j * (width // 8), width // 2 + j * (width // 4) + x * (width // 8)
 
 
-def cut_count(slots):
-    return 5 if slots % 5 == 0 else 1
+def cut_count(slots, finer=1):
+    for cuts in (5 * finer, 5):
+        if slots % cuts == 0:
+            return cuts
+    return 1
 
 
 def gather_grid_kernel(n, slots, grid_qkv, grid_out, slot_ref, w_ref, p_ref, tokens_ref, gain_ref,
@@ -1393,7 +1396,7 @@
         device_id_type=pl.DeviceIdType.MESH,
     )
     swap.start()
-    cuts = cut_count(slots)
+    cuts = cut_count(slots, 2)
     size = slots // cuts
     rows, cols = grid_qkv
     out_rows, out_cols = grid_out
@@ -1401,7 +1404,7 @@
     edge = out_ref.shape[-1]
     legs = core_send.shape[0] - out_rows
     leg_rows = rows // 2 // legs
-    group = 2
+    group = 4
     giver = 1 - lax.rem(z, 2)
 
     def core_copy(i):
@@ -1618,7 +1621,7 @@
     slots = picked.shape[0] // n
     edge = BLK
     total_blocks = grid_qkv[0] * grid_qkv[1] + grid_out[0] * grid_out[1]
-    cuts = cut_count(slots)
+    cuts = cut_count(slots, 2)
     legs = 4
     vmem = pl.BlockSpec(memory_space=pltpu.VMEM)
     dma = pltpu.SemaphoreType.DMA

time: 356 us -> 355 us (level)
  no operation moved by 1% of the time
where the time goes in v6:
time: 355 us; the launch traced here: 354 us
  Pallas kernels  348 us (98%)
  other arithmetic  5.19 us (1%)
    pallas_call x1, Pallas kernels, gather_grid(): pl.pallas_call(functools.partial(gather_grid_kernel, n, slots, grid_qkv,...  170 us
    pallas_call x1, Pallas kernels, reduce_grid(): pl.pallas_call(functools.partial(reduce_grid_kernel, n, slots, grid_qkv,...  93.3 us
    pallas_call x1, Pallas kernels, square_exchange(): pl.pallas_call(functools.partial(square_kernel, heads), out_shape=(jax.Sh...  84.3 us
  transfers between devices with their start and end apart: 1, of which 1 were waited for; matrix products, arithmetic and copies ran while one was open for 0% of the time, Pallas kernels for 0%

profile of v6, /device:TPU:1, one launch (start us, length us, event | category | flops | bytes accessed | tf_op | source)
XLA Modules:
  0.0 354.3 jit_solution(3990300268201136582)
XLA Ops:
  0.0 0.0 collective-permute-start
  0.0 1.3 collective-permute-done
  1.3 0.2 reduce-window.4
  1.5 0.1 convert_reduce_fusion
  1.6 0.1 select_reduce_fusion.2
  1.7 0.6 add_subtract_fusion.slot_ref
  2.3 0.1 select_reduce_fusion.1
  2.3 0.6 add_select_fusion.2.pick_ref
  2.9 170.2 %shard_map.82 = (f32[512,768]{1,0:T(8,128)}, f32[512,768]{1,0:T(8,128)}, bf16[512,4096]{1,0:T(8,128)(2,1)}, bf16[512,4096]{1,0:T(8,128)(2,1)}, bf16[2048,1024]{1,0:T(8,128)(2,1)}, /*index=5*/bf16[2,512,512]{2,1,0:T(8,128)(2,1)}) custom-call(s32[320]{0:T(512)} %add_subtract_fusion.slot_ref, bf16[50,128,128]{2,1,0:T(8,128)(2,1)} %bitcast.18, ...), custom_call_target="tpu_custom_call" | custom-call | tf_op jit(solution)/shard_map/pallas_call | solution.py:977
  173.1 84.3 %shard_map.83 = (bf16[1024,2048]{1,0:T(8,128)(2,1)}, bf16[512,768]{1,0:T(8,128)(2,1)}, bf16[512,1024]{1,0:T(8,128)(2,1)}) custom-call(f32[512,768]{1,0:T(8,128)} %get-tuple-element.15.proj_ref, f32[512,768]{1,0:T(8,128)} %get-tuple-element.16.d_proj_ref, bf16[512,4096]{1,0:T(8,128)(2,1)} %get-tuple-element.17.w_out, ...), custom_call_target="tpu_custom_call" | custom-call | tf_op jit(solution)/shard_map/pallas_call | solution.py:1337
  257.5 93.3 %shard_map.84 = bf16[50,128,128]{2,1,0:T(8,128)(2,1)} custom-call(s32[400]{0:T(512)} %add_select_fusion.2.pick_ref, bf16[2048,1024]{1,0:T(8,128)(2,1)} %get-tuple-element.14.normed_t_in, bf16[512,768]{1,0:T(8,128)(2,1)} %get-tuple-element.20.d_proj_in, bf16[512,1024]{1,0:T(8,128)(2,1)} %get-tuple-element.21.mixed_t_ref, ...), custom_call_target="tpu_custom_call" | custom-call | tf_op jit(solution)/shard_map/pallas_call | solution.py:1628
  350.8 3.5 %multiply_bitcast_fusion = f32[1,50,128,128]{3,2,1,0:T(8,128)} fusion(bf16[50,128,128]{2,1,0:T(8,128)(2,1)} %shard_map.84), kind=kLoop, calls=%fused_computation | loop fusion | flops 1638400 | bytes 4915200 | tf_op jit(solution)/shard_map/mul | solution.py:1713
  (3 shorter events, 0.0 us)
Async XLA Ops:
  0.0 1.3 collective-permute-start
